TPU v7x, 256 devices: a whole 4x4x8 slice. The times are simulated.
256 devices in a mesh: fiber: 128 (over z, y, x), wave: 2 (over core).
Axes of the slice: x: 4, y: 4, z: 8, core: 2. Of those that a mesh axis runs over, the one named last changes fastest.
Arguments:
- spectra: float32 [4, 5120, 8192], P(None, 'fiber', 'wave'), may hold values from 0 to 10
- inverse_var: float32 [4, 5120, 8192], P(None, 'fiber', 'wave'), may hold values from 0.1 to 10
- mask_bits: int32 [4, 5120, 8192], P(None, 'fiber', 'wave'), may hold values from 0 to 512, as said below
- sky_flags: int32 [4, 5120], P(None, 'fiber'), may hold values 0 or 1
- fiber_ids: int32 [5120], P('fiber'), may hold values from 0 to 5119, each once
- positions: float32 [2, 5120], replicated, may hold values from -1 to 1
- throughput: float32 [4, 5120], P(None, 'fiber'), may hold values from 0.5 to 1.5
Outputs:
- residual: float32 [4, 5120, 8192], P(None, 'fiber', 'wave')
- chi_square: float32 [4, 5120], P(None, 'fiber')
- sky_coeffs: float32 [16, 8192], P(None, 'wave')
Inputs may be any that keep to these rules, and one draw needn't show every extreme that they name: `mask_bits`: each entry is zero or one single bit of 0 to 9. `fiber_ids`: each fiber id appears in exactly one slot.
All inputs are finite; a program needn't handle non-finite values. No bound on the sum of `sky_flags` on one device may be relied on, other than what follows from the above.
Results may differ from a plain program's by a relative error of at most 0.0003.
Values sent between devices are 32-bit elements; how exact they have to be, the bound alone decides.
No kernel may reach another device: no remote copies, remote signals or barrier semaphores. Data moves between devices by JAX's collectives and lax.ppermute only.
A program may use at most 64 MiB of HBM per device.

v0:
```python
import jax
import jax.numpy as jnp
from jax import lax
from jax.sharding import PartitionSpec as P

PARAMS = 16


bad_bits = 31
prior_weight = 1.0
highest = lax.Precision.HIGHEST
moment_degrees = 7
basis_degrees = 4


def over_pieces(value, axis):
    return lax.all_gather(value, axis).sum(0)


def legendre(coord):
    return [
        jnp.ones_like(coord),
        coord,
        1.5 * coord * coord - 0.5,
        (2.5 * coord * coord - 1.5) * coord,
    ]


def legendre_series(coord, degree_total):
    series = [jnp.ones_like(coord), coord]
    for order in range(1, degree_total - 1):
        series.append(
            ((2 * order + 1) * coord * series[order] - order * series[order - 1]) / (order + 1)
        )
    return series


def build_design(positions, fiber_ids, throughput):
    coord_x = positions[0][fiber_ids]
    coord_y = positions[1][fiber_ids]
    poly_x = legendre(coord_x)
    poly_y = legendre(coord_y)
    basis = jnp.stack([along_x * along_y for along_x in poly_x for along_y in poly_y], axis=-1)
    return throughput[:, :, None] * basis[None]


def moment_features(positions, fiber_ids, throughput):
    coord_x = positions[0][fiber_ids]
    coord_y = positions[1][fiber_ids]
    series_x = legendre_series(coord_x, moment_degrees)
    series_y = legendre_series(coord_y, moment_degrees)
    basis = jnp.stack([along_x * along_y for along_x in series_x for along_y in series_y], axis=-1)
    return (throughput * throughput)[:, :, None] * basis[None]


def monomial_table(degree_total):
    coeffs = [[0.0] * degree_total for order in range(degree_total)]
    coeffs[0][0] = 1.0
    coeffs[1][1] = 1.0
    for order in range(1, degree_total - 1):
        for power in range(degree_total):
            raised = coeffs[order][power - 1] if power >= 1 else 0.0
            coeffs[order + 1][power] = (
                (2 * order + 1) * raised - order * coeffs[order - 1][power]
            ) / (order + 1)
    return coeffs


def product_series(higher, first, second):
    product = [0.0] * moment_degrees
    for left_power in range(moment_degrees):
        for right_power in range(moment_degrees - left_power):
            product[left_power + right_power] += (
                higher[first][left_power] * higher[second][right_power]
            )
    series = [0.0] * moment_degrees
    for order in reversed(range(moment_degrees)):
        weight_now = product[order] / higher[order][order]
        series[order] = weight_now
        for power in range(moment_degrees):
            product[power] -= weight_now * higher[order][power]
    return series


def rebuild_table():
    higher = monomial_table(moment_degrees)
    pair_coeffs = [
        [product_series(higher, first, second) for second in range(basis_degrees)]
        for first in range(basis_degrees)
    ]
    table_rows = []
    for index_i in range(basis_degrees):
        for index_j in range(basis_degrees):
            for index_k in range(basis_degrees):
                for index_l in range(basis_degrees):
                    table_rows.append(
                        [
                            pair_coeffs[index_i][index_k][order_a]
                            * pair_coeffs[index_j][index_l][order_b]
                            for order_a in range(moment_degrees)
                            for order_b in range(moment_degrees)
                        ]
                    )
    return jnp.asarray(table_rows, jnp.float32)


def solve_normal(matrix, right_side):
    param_count = right_side.shape[0]
    factor = {}
    for column in range(param_count):
        pivot_sum = matrix[column * param_count + column] + prior_weight
        for inner_k in range(column):
            pivot_sum = pivot_sum - factor[column, inner_k] * factor[column, inner_k]
        root_value = jnp.sqrt(pivot_sum)
        factor[column, column] = root_value
        for target in range(column + 1, param_count):
            running = matrix[target * param_count + column]
            for inner_k in range(column):
                running = running - factor[target, inner_k] * factor[column, inner_k]
            factor[target, column] = running / root_value
    interim = []
    for target in range(param_count):
        running = right_side[target]
        for inner_k in range(target):
            running = running - factor[target, inner_k] * interim[inner_k]
        interim.append(running / factor[target, target])
    solved = [None] * param_count
    for target in reversed(range(param_count)):
        running = interim[target]
        for inner_k in range(target + 1, param_count):
            running = running - factor[inner_k, target] * solved[inner_k]
        solved[target] = running / factor[target, target]
    return jnp.stack(solved)


def expand_normal(normal):
    return jnp.dot(rebuild_table(), normal, precision=highest)


def body(spectra, inverse_var, mask_bits, sky_flags, fiber_ids, positions, throughput):
    exposures, fiber_count, wave_count = spectra.shape
    row_count = exposures * fiber_count
    design = build_design(positions, fiber_ids, throughput).reshape(row_count, PARAMS)
    flux_rows = spectra.reshape(row_count, wave_count)
    usable = (mask_bits.reshape(row_count, wave_count) & bad_bits == 0).astype(jnp.float32)
    noise_weight = inverse_var.reshape(row_count, wave_count) * usable
    fit_weights = noise_weight * sky_flags.reshape(row_count).astype(jnp.float32)[:, None]
    products = moment_features(positions, fiber_ids, throughput).reshape(
        row_count, moment_degrees * moment_degrees
    )
    normal = jnp.dot(products.T, fit_weights, precision=highest)
    right_side = jnp.dot(design.T, fit_weights * flux_rows, precision=highest)
    normal, right_side = lax.psum((normal, right_side), "fiber")
    normal = expand_normal(normal)
    sky_coeffs = solve_normal(normal, right_side)
    residual = flux_rows - jnp.dot(design, sky_coeffs, precision=highest)
    chi_local = jnp.sum(noise_weight * residual * residual, axis=1)
    chi_total = over_pieces(chi_local, "wave")
    chi_square = (chi_total / (wave_count * lax.axis_size("wave"))).reshape(exposures, fiber_count)
    return (residual.reshape(exposures, fiber_count, wave_count), chi_square, sky_coeffs)


def solution(mesh):
    placed = (
        P(None, "fiber", "wave"),
        P(None, "fiber", "wave"),
        P(None, "fiber", "wave"),
        P(None, "fiber"),
        P("fiber"),
        P(),
        P(None, "fiber"),
    )
    return jax.shard_map(
        body,
        mesh=mesh,
        in_specs=placed,
        out_specs=(P(None, "fiber", "wave"), P(None, "fiber"), P(None, "wave")),
        check_vma=False,
    )
```

profile of v0, /device:TPU:1, one launch (start us, length us, event | category | flops | bytes accessed | tf_op | source)
XLA Modules:
  0.0 298.1 jit_solution(2693656242607218048)
XLA Ops:
  7.2 0.0 all-reduce.4.cloned.1.call-start
  7.2 0.9 fusion.83
  8.1 0.7 compare_select_fusion
  8.8 0.8 gather_fusion
  9.5 0.8 gather_fusion.1
  10.3 0.8 mul.18449
  11.1 0.1 stack.18
  11.2 0.7 broadcast_multiply_fusion
  11.9 0.7 convert_element_type.8
  12.6 0.1 stack.19
  12.7 0.1 copy.15
  12.8 3.0 %fusion.2 = f32[4,40,4096]{2,1,0:T(8,128)S(1)} fusion(f32[4,40,4096]{2,1,0:T(8,128)} %param.9, s32[4,40,4096]{2,1,0:T(8,128)} %param.10), kind=kLoop, calls=%fused_computation.9 | loop fusion | flops 1966080 | bytes 7864320 | tf_op jit(solution)/shard_map/mul | solution.py:146
  15.8 0.3 copy-done
  16.1 2.6 convolution_bitcast_fusion.1
  18.7 2.7 convolution_bitcast_fusion
  21.3 0.0 all-reduce.4.cloned.1.call-update
  21.3 0.0 copy-done.4
  21.3 0.1 mul.18419
  21.4 0.1 mul.18441
  21.5 0.6 dynamic-slice
  22.8 220.4 %all-reduce.4.cloned.1.call-done = (f32[49,4096]{1,0:T(8,128)}, f32[16,4096]{1,0:T(8,128)}) async-done(((f32[49,4096]{1,0:T(8,128)}, f32[16,4096]{1,0:T(8,128)}), (f32[49,4096]{1,0:T(8,128)}, f32[16,4096]{1,0:T(8,128)})) %all-reduce.4.cloned.1.call-update) | async-done | bytes 1064976 | tf_op jit(solution)/shard_map/psum | solution.py:153
  243.2 4.6 %fusion.84 = f32[256,4096]{1,0:T(8,128)S(1)} fusion(f32[256,49]{1,0:T(8,128)S(1)} %copy-done.3, f32[49,4096]{1,0:T(8,128)} %get-tuple-element.3), kind=kOutput, calls=%fused_computation.467 | convolution fusion | flops 616562688 | bytes 5047296 | tf_op jit(solution)/shard_map/dot_general | solution.py:137
  247.8 1.4 subtract_divide_fusion.104
  249.2 0.1 slice_divide_fusion.7
  249.4 0.2 fusion.77
  249.6 0.2 fusion.76
  249.8 0.3 fusion.78
  250.1 0.3 fusion.75
  250.4 0.3 fusion.79
  250.7 0.3 fusion.80
  251.0 0.2 fusion.81
  251.2 0.0 copy-done.1
  251.2 0.2 fusion.82
  251.4 2.1 subtract_divide_fusion.143
  253.6 1.4 subtract_divide_fusion.144
  255.0 1.4 subtract_divide_fusion.145
  256.4 1.9 subtract_divide_fusion.133
  258.4 1.7 subtract_divide_fusion.131
  260.0 10.1 %subtract_divide_fusion.26 = (f32[1,4096]{1,0:T(1,128)S(1)}, f32[1,4096]{1,0:T(1,128)S(1)}, f32[1,4096]{1,0:T(1,128)S(1)}, f32[1,4096]{1,0:T(1,128)S(1)}, f32[1,...) fusion(f32[16,4096]{1,0:T(8,128)S(1)} %copy-done.1, ...), kind=kLoop, calls=%fused_computation.63 | loop fusion | flops 5423104 | bytes 3751936 | tf_op jit(solution)/shard_map/div | solution.py:126
  270.2 3.2 %subtract_divide_fusion.12 = (f32[1,4096]{1,0:T(1,128)S(1)}, f32[1,4096]{1,0:T(1,128)S(1)}, f32[1,4096]{1,0:T(1,128)S(1)}, f32[1,4096]{1,0:T(1,128)S(1)}, f32[1,...) fusion(f32[1,4096]{1,0:T(1,128)S(1)} %get-tuple-element.33, ...), kind=kLoop, calls=%fused_computation.48 | loop fusion | flops 1511424 | bytes 2457600 | tf_op jit(solution)/shard_map/div | solution.py:120
  273.3 3.2 %subtract_divide_fusion = (f32[1,4096]{1,0:T(1,128)S(1)}, f32[1,4096]{1,0:T(1,128)S(1)}, f32[1,4096]{1,0:T(1,128)S(1)}, f32[1,4096]{1,0:T(1,128)S(1)}, f32[1,409...) fusion(f32[1,4096]{1,0:T(1,128)S(1)} %get-tuple-element.123, ...), kind=kLoop, calls=%fused_computation.35 | loop fusion | flops 1499136 | bytes 2457600 | tf_op jit(solution)/shard_map/div | solution.py:132
  276.5 0.4 stack.23
  276.9 0.0 copy-start.2
  276.9 5.8 %fusion = (f32[160]{0:T(256)S(1)}, f32[160,4096]{1,0:T(8,128)}) fusion(f32[160,4096]{1,0:T(8,128)S(1)} %bitcast.382, f32[160,4096]{1,0:T(8,128)} %bitcast.385, f32[16,4096]{1,0:T(8,128)S(1)} %stack.23, f32[160,16]{0,1:T(8,128)S(1)} %mul.18441, f32[160]{0:T(256)S(1)} %mul.18419), kind=kOutput, calls=%fused_computation.6 | convolution fusion | flops 128452960 | bytes 8137984 | tf_op jit(solution)/shard_map/dot_general | solution.py:156
  282.8 0.2 dynamic-update-slice
  283.0 7.5 %all-reduce = f32[320]{0:T(512)S(1)} all-reduce(f32[320]{0:T(512)S(1)} %dynamic-update-slice), channel_id=2, replica_groups=mesh['fiber'=128,'wave'=2] {'wave'}, use_global_device_ids=true, to_apply=%add | all-reduce | flops 320 | bytes 2560
  290.4 0.1 reshape.842
  290.6 0.7 div.2945
  (15 shorter events, 0.1 us)
Async XLA Ops:
  7.2 236.0 %all-reduce.4.cloned.1.call-start = ((), (), s32[]{:S(2)}) async-start(), calls=%async_computation | async-start | bytes 2359296 | tf_op jit(solution)/shard_map/psum | solution.py:153
  12.8 3.3 %copy-start = (f32[4,40,4096]{2,1,0:T(8,128)S(1)}, f32[4,40,4096]{2,1,0:T(8,128)}, u32[]{:S(2)}) copy-start(f32[4,40,4096]{2,1,0:T(8,128)} %param.8) | copy-start | bytes 7864324
  18.6 2.7 copy-start.4
  18.6 2.9 copy-start.5
  18.6 224.5 %copy-start.3 = (f32[256,49]{1,0:T(8,128)S(1)}, f32[256,49]{1,0:T(8,128)}, u32[]{:S(2)}) copy-start(f32[256,49]{1,0:T(8,128)} %constant.70.clone) | copy-start | bytes 150532
  247.8 3.4 %copy-start.1 = (f32[16,4096]{1,0:T(8,128)S(1)}, f32[16,4096]{1,0:T(8,128)}, u32[]{:S(2)}) copy-start(f32[16,4096]{1,0:T(8,128)} %get-tuple-element.4) | copy-start | bytes 786436
  276.9 5.8 %copy-start.2 = (f32[16,4096]{1,0:T(8,128)}, f32[16,4096]{1,0:T(8,128)S(1)}, u32[]{:S(2)}) copy-start(f32[16,4096]{1,0:T(8,128)S(1)} %stack.23) | copy-start | bytes 786436
Sparse Core Ops, SparseCore 0:
  21.5 221.6 all-reduce.3
where the time goes:
time: 298 us
  waiting for transfers between devices  220 us (74%)
  other arithmetic  34.3 us (12%)
  matrix products  15.7 us (5%)
  between operations  14.9 us (5%)
  blocking collectives  7.46 us (3%)
  local copies, waits for them, and re-layouts  5.33 us (2%)
    psum x1, waiting for transfers between devices, body(): normal, right_side = lax.psum((normal, right_side), 'fiber')  220 us
    div x6, other arithmetic, solve_normal(): solved[target] = running / factor[target, target]  11.8 us
    div x1, other arithmetic, solve_normal(): interim.append(running / factor[target, target])  10.1 us
    unnamed x1, blocking collectives  7.46 us
  transfers between devices with their start and end apart: 1, of which 1 were waited for; matrix products, arithmetic and copies ran while one was open for 0% of the time, Pallas kernels for 0%

commit v1 on v0

v1 whole, which is shorter than its diff:
```python
import functools

import jax
import jax.numpy as jnp
from jax import lax
from jax.experimental import pallas as pl
from jax.experimental.pallas import tpu as pltpu
from jax.sharding import PartitionSpec as P

PARAMS = 16
BAD_BITS = 31
PRIOR = 1.0
MOMENTS = 7
BASIS = 4
RIGHT_ROW = 56
PACKED = 72
LANES = 128
BLOCK = 512


def legendre_series(coord, total):
    series = [jnp.ones_like(coord), coord]
    for order in range(1, total - 1):
        series.append(((2 * order + 1) * coord * series[order] - order * series[order - 1]) / (order + 1))
    return series


def monomial_table(total):
    coeffs = [[0.0] * total for _ in range(total)]
    coeffs[0][0] = 1.0
    coeffs[1][1] = 1.0
    for order in range(1, total - 1):
        for power in range(total):
            raised = coeffs[order][power - 1] if power >= 1 else 0.0
            coeffs[order + 1][power] = ((2 * order + 1) * raised - order * coeffs[order - 1][power]) / (order + 1)
    return coeffs


def product_series(higher, first, second):
    product = [0.0] * MOMENTS
    for left in range(MOMENTS):
        for right in range(MOMENTS - left):
            product[left + right] += higher[first][left] * higher[second][right]
    series = [0.0] * MOMENTS
    for order in reversed(range(MOMENTS)):
        now = product[order] / higher[order][order]
        series[order] = now
        for power in range(MOMENTS):
            product[power] -= now * higher[order][power]
    return series


def rebuild_rows():
    higher = monomial_table(MOMENTS)
    pair = [[product_series(higher, a, b) for b in range(BASIS)] for a in range(BASIS)]
    rows = []
    for i in range(BASIS):
        for j in range(BASIS):
            for k in range(BASIS):
                for l in range(BASIS):
                    row = [0.0] * LANES
                    for a in range(MOMENTS):
                        for b in range(MOMENTS):
                            row[a * MOMENTS + b] = pair[i][k][a] * pair[j][l][b]
                    rows.append(row)
    return rows


def split3(value):
    high = value.astype(jnp.bfloat16)
    rest = value - high.astype(jnp.float32)
    middle = rest.astype(jnp.bfloat16)
    low = (rest - middle.astype(jnp.float32)).astype(jnp.bfloat16)
    return high, middle, low


def dot6(left, right):
    l1, l2, l3 = split3(left)
    r1, r2, r3 = split3(right)
    total = None
    for a, b in ((l1, r3), (l3, r1), (l2, r2), (l1, r2), (l2, r1), (l1, r1)):
        part = jnp.dot(a, b, preferred_element_type=jnp.float32)
        total = part if total is None else total + part
    return total


def moments_kernel(ids_ref, pos_ref, tput_ref, sky_ref, flux_ref, ivar_ref, bits_ref, out_ref, feat_ref, small_ref, stack_ref, left_ref):
    fibers = flux_ref.shape[1]
    exposures = flux_ref.shape[0]

    @pl.when(pl.program_id(0) == 0)
    def _():
        stack_ref[...] = jnp.zeros_like(stack_ref)
        stack_ref[0:exposures, 0:fibers] = tput_ref[...]
        stack_ref[8:8 + exposures, 0:fibers] = sky_ref[...].astype(jnp.float32)
        turned = stack_ref[0:LANES, :].T
        sub = lax.broadcasted_iota(jnp.int32, (fibers, LANES), 0)
        lane = lax.broadcasted_iota(jnp.int32, (fibers, LANES), 1)
        ids = jnp.zeros((fibers, LANES), jnp.int32)
        for f in range(fibers):
            ids = jnp.where(sub == f, ids_ref[f], ids)
        sum_x = jnp.zeros((fibers, LANES), jnp.float32)
        sum_y = jnp.zeros((fibers, LANES), jnp.float32)
        offset = ids - lane
        for tile in range(pos_ref.shape[1] // LANES):
            hit = offset == tile * LANES
            cut = slice(tile * LANES, (tile + 1) * LANES)
            sum_x = jnp.where(hit, pos_ref[0:1, cut], sum_x)
            sum_y = jnp.where(hit, pos_ref[1:2, cut], sum_y)
        coord_x = jnp.sum(sum_x, axis=1, keepdims=True)
        coord_y = jnp.sum(sum_y, axis=1, keepdims=True)
        series_x = legendre_series(jnp.broadcast_to(coord_x, (fibers, LANES)), MOMENTS)
        series_y = legendre_series(jnp.broadcast_to(coord_y, (fibers, LANES)), MOMENTS)
        is_right = lane >= RIGHT_ROW
        index_x = jnp.where(is_right, (lane - RIGHT_ROW) // BASIS, lane // MOMENTS)
        index_y = jnp.where(is_right, (lane - RIGHT_ROW) % BASIS, lane % MOMENTS)
        along_x = jnp.zeros((fibers, LANES), jnp.float32)
        along_y = jnp.zeros((fibers, LANES), jnp.float32)
        for order in range(MOMENTS):
            along_x = jnp.where(index_x == order, series_x[order], along_x)
            along_y = jnp.where(index_y == order, series_y[order], along_y)
        product = along_x * along_y
        moment_part = jnp.where(lane < MOMENTS * MOMENTS, product, 0.0)
        right_part = jnp.where(is_right & (lane < RIGHT_ROW + PARAMS), product, 0.0)
        feat_ref[0:fibers, :] = right_part
        feat_ref[fibers:2 * fibers, :] = turned[0:fibers, :]
        small_ref[...] = turned[0:fibers, :]
        both = jnp.concatenate([moment_part, right_part], axis=0)
        high, middle, low = (part.astype(jnp.float32) for part in split3(both))
        rows = 2 * fibers
        for place, part in enumerate((high, middle, low, high, middle, high)):
            stack_ref[place * rows:(place + 1) * rows, :] = part
        stack_ref[6 * rows:, :] = jnp.zeros((stack_ref.shape[0] - 6 * rows, LANES), jnp.float32)
        for tile in range(stack_ref.shape[0] // LANES):
            cut = slice(tile * LANES, (tile + 1) * LANES)
            left_ref[:, cut] = stack_ref[cut, :].T[0:left_ref.shape[0], :].astype(jnp.bfloat16)

    columns = small_ref[...]
    moment_rows = None
    right_rows = None
    for e in range(exposures):
        through = columns[:, e:e + 1]
        sky = columns[:, 8 + e:9 + e]
        weight = jnp.where((bits_ref[e] & BAD_BITS) == 0, ivar_ref[e], 0.0)
        first = weight * (through * sky)
        a = first * through
        b = first * flux_ref[e]
        moment_rows = a if e == 0 else moment_rows + a
        right_rows = b if e == 0 else right_rows + b
    high, middle, low = split3(jnp.concatenate([moment_rows, right_rows], axis=0))
    right = jnp.concatenate([high, high, high, middle, middle, low], axis=0)
    sums = jnp.dot(left_ref[:, 0:right.shape[0]], right, preferred_element_type=jnp.float32)
    for k in range(out_ref.shape[0]):
        out_ref[k] = sums[0:PACKED, k * LANES:(k + 1) * LANES]


def add_kernel(in_ref, out_ref):
    total = in_ref[0]
    for source in range(1, in_ref.shape[0]):
        total = total + in_ref[source]
    for target in range(out_ref.shape[0]):
        out_ref[target] = total


def solve_kernel(in_ref, table_ref, out_ref):
    total = in_ref[0]
    for source in range(1, in_ref.shape[0]):
        total = total + in_ref[source]
    moments = jnp.concatenate([total[0:RIGHT_ROW], jnp.zeros((LANES - RIGHT_ROW, LANES), jnp.float32)], axis=0)
    normal = dot6(table_ref[...], moments)
    sub = lax.broadcasted_iota(jnp.int32, (PARAMS, LANES), 0)
    columns = []
    for k in range(PARAMS):
        column = normal[k * PARAMS:(k + 1) * PARAMS]
        columns.append(jnp.where(sub == k, column + PRIOR, column))
    right = total[RIGHT_ROW:RIGHT_ROW + PARAMS]
    scale = jnp.zeros((PARAMS, LANES), jnp.float32)
    for j in range(PARAMS):
        inverse = 1.0 / columns[j][j:j + 1]
        scale = jnp.where(sub == j, inverse, scale)
        factor = jnp.where(sub == j, 0.0, columns[j] * inverse)
        for l in range(j + 1, PARAMS):
            columns[l] = columns[l] - factor * columns[l][j:j + 1]
        right = right - factor * right[j:j + 1]
    right = right * scale
    for target in range(out_ref.shape[0]):
        out_ref[target] = right


def residual_kernel(feat_ref, coeff_ref, flux_ref, ivar_ref, bits_ref, res_ref, all_ref, chi_ref, sum_ref):
    step = pl.program_id(0)
    exposures, fibers, width = flux_ref.shape

    @pl.when(step == 0)
    def _():
        sum_ref[...] = jnp.zeros_like(sum_ref)

    coeffs = jnp.concatenate([coeff_ref[k] for k in range(coeff_ref.shape[0])], axis=1)
    all_ref[...] = coeffs
    basis = feat_ref[0:fibers, RIGHT_ROW:RIGHT_ROW + PARAMS]
    model = dot6(basis, coeffs)
    for e in range(exposures):
        through = feat_ref[fibers:2 * fibers, e:e + 1]
        residual = flux_ref[e] - through * model
        res_ref[e] = residual
        weight = jnp.where((bits_ref[e] & BAD_BITS) == 0, ivar_ref[e], 0.0)
        chi = weight * residual * residual
        part = chi[:, 0:LANES]
        for k in range(1, width // LANES):
            part = part + chi[:, k * LANES:(k + 1) * LANES]
        sum_ref[e * fibers:(e + 1) * fibers, :] += part

    @pl.when(step == pl.num_programs(0) - 1)
    def _():
        ones = jnp.ones((8, LANES), jnp.float32)
        chi_ref[...] = lax.dot_general(ones, sum_ref[...], (((1,), (1,)), ((), ())), precision=lax.Precision.HIGHEST, preferred_element_type=jnp.float32)


def chi_kernel(scale, mine_ref, other_ref, out_ref):
    exposures, fibers = out_ref.shape
    total = (mine_ref[...] + other_ref[...]) * scale
    for e in range(exposures):
        out_ref[e:e + 1, :] = total[0:1, e * fibers:(e + 1) * fibers]


def vmem(*shape):
    return pl.BlockSpec(shape, lambda *_: (0,) * len(shape))


def cost(flops, moved):
    return pl.CostEstimate(flops=flops, bytes_accessed=moved, transcendentals=0)


def params(limit_mib, dims=0):
    semantics = {"dimension_semantics": ("arbitrary",) * dims} if dims else {}
    return pltpu.CompilerParams(vmem_limit_bytes=limit_mib * 1024 * 1024, **semantics)


def groups(sizes):
    nz, ny, nx = sizes

    def place(z, y, x):
        return (z * ny + y) * nx + x

    pair = 2
    near = [[place(q * pair + h, y, x) for h in range(pair) for y in range(ny) for x in range(nx)] for q in range(nz // pair)]
    far = [[place(q * pair + h, y, x) for q in range(nz // pair)] for h in range(pair) for y in range(ny) for x in range(nx)]
    return near, far


def make_body(near, far):
    def body(spectra, inverse_var, mask_bits, sky_flags, fiber_ids, positions, throughput):
        exposures, fibers, waves = spectra.shape
        steps = waves // BLOCK
        per_step = BLOCK // LANES
        f32 = jnp.float32
        wide = pl.BlockSpec((exposures, fibers, BLOCK), lambda s: (0, 0, s))
        stacked = -(-12 * fibers // LANES) * LANES

        packed, feats = pl.pallas_call(
            moments_kernel,
            grid=(steps,),
            in_specs=[
                pl.BlockSpec(memory_space=pltpu.SMEM),
                vmem(*positions.shape),
                vmem(exposures, fibers),
                vmem(exposures, fibers),
                wide, wide, wide,
            ],
            out_specs=[
                pl.BlockSpec((per_step, PACKED, LANES), lambda s: (s, 0, 0)),
                vmem(2 * fibers, LANES),
            ],
            out_shape=[
                jax.ShapeDtypeStruct((waves // LANES, PACKED, LANES), f32),
                jax.ShapeDtypeStruct((2 * fibers, LANES), f32),
            ],
            scratch_shapes=[
                pltpu.VMEM((fibers, LANES), f32),
                pltpu.VMEM((stacked, LANES), f32),
                pltpu.VMEM((80, stacked), jnp.bfloat16),
            ],
            compiler_params=params(16, 1),
            cost_estimate=cost(2 * 6 * PACKED * 2 * fibers * waves, 3 * 4 * exposures * fibers * waves),
            name="moments",
        )(fiber_ids, positions, throughput, sky_flags, spectra, inverse_var, mask_bits)

        arrived = lax.all_to_all(packed, "fiber", 0, 0, axis_index_groups=near, tiled=True)
        copies = pl.pallas_call(
            add_kernel,
            out_shape=jax.ShapeDtypeStruct((len(far[0]), PACKED, LANES), f32),
            compiler_params=params(8),
            name="add",
        )(arrived)
        parts = lax.all_to_all(copies, "fiber", 0, 0, axis_index_groups=far, tiled=True)
        solved = pl.pallas_call(
            solve_kernel,
            out_shape=jax.ShapeDtypeStruct((len(near[0]), PARAMS, LANES), f32),
            compiler_params=params(8),
            name="solve",
        )(parts, jnp.asarray(rebuild_rows(), f32))
        coeffs = lax.all_to_all(solved, "fiber", 0, 0, axis_index_groups=near, tiled=True)

        residual, sky_coeffs, chi_local = pl.pallas_call(
            residual_kernel,
            grid=(steps,),
            in_specs=[
                vmem(2 * fibers, LANES),
                pl.BlockSpec((per_step, PARAMS, LANES), lambda s: (s, 0, 0)),
                wide, wide, wide,
            ],
            out_specs=[
                wide,
                pl.BlockSpec((PARAMS, BLOCK), lambda s: (0, s)),
                vmem(8, exposures * fibers),
            ],
            out_shape=[
                jax.ShapeDtypeStruct(spectra.shape, f32),
                jax.ShapeDtypeStruct((PARAMS, waves), f32),
                jax.ShapeDtypeStruct((8, exposures * fibers), f32),
            ],
            scratch_shapes=[pltpu.VMEM((exposures * fibers, LANES), f32)],
            compiler_params=params(16, 1),
            cost_estimate=cost(2 * 6 * PARAMS * fibers * waves, 4 * 4 * exposures * fibers * waves),
            name="residual",
        )(feats, coeffs, spectra, inverse_var, mask_bits)

        halves = lax.axis_size("wave")
        chi_other = lax.ppermute(chi_local, "wave", [(h, (h + 1) % halves) for h in range(halves)])
        chi_square = pl.pallas_call(
            functools.partial(chi_kernel, 1.0 / (waves * halves)),
            out_shape=jax.ShapeDtypeStruct((exposures, fibers), f32),
            compiler_params=params(4),
            name="chi",
        )(chi_local, chi_other)
        return residual, chi_square, sky_coeffs

    return body


def solution(mesh):
    near, far = groups((8, 4, 4))
    placed = (
        P(None, "fiber", "wave"),
        P(None, "fiber", "wave"),
        P(None, "fiber", "wave"),
        P(None, "fiber"),
        P("fiber"),
        P(),
        P(None, "fiber"),
    )
    return jax.shard_map(
        make_body(near, far),
        mesh=mesh,
        in_specs=placed,
        out_specs=(P(None, "fiber", "wave"), P(None, "fiber"), P(None, "wave")),
        check_vma=False,
    )
```

time: 298 us -> 79.8 us (0.27)
  waiting for transfers between devices: 220 us -> 0.83 us
  blocking collectives: 7.46 us -> 54.2 us
  other arithmetic: 34.3 us -> 0 us
  matrix products: 15.7 us -> 0 us
  between operations: 14.9 us -> 0.69 us
  Pallas kernels: 0 us -> 11.3 us
  starting transfers between devices: 0.04 us -> 4.34 us
    psum x1 -> x0, waiting for transfers between devices: 220 us -> none  [body(): normal, right_side = lax.psum((normal, right_side), 'fiber')]
    all_to_all x0 -> x3, blocking collectives: none -> 54.2 us  [the longest x1 27.3 us: body(): lax.all_to_all(packed, 'fiber', 0, 0, axis_index_groups=near, tiled=True)]
    div x11 -> x0, other arithmetic: 26.6 us -> none  [the longest x6 11.8 us: solve_normal(): solved[target] = running / factor[target, target]]
    dot_general x4 -> x0, matrix products: 15.7 us -> none  [the longest x1 5.83 us: body(): residual = flux_rows - jnp.dot(design, sky_coeffs, precision=highest)]
    pallas_call x0 -> x5, Pallas kernels: none -> 11.3 us  [the longest x1 5.35 us: body(): pl.pallas_call(residual_kernel, grid=(steps,), in_specs=[vmem(2 * fibers,...]
    unnamed x1 -> x0, blocking collectives: 7.46 us -> none
    unnamed x15 -> x22, local copies, waits for them, and re-layouts: 1.09 us -> 8.03 us
    mul x4 -> x0, other arithmetic: 4.51 us -> none  [the longest x1 3.03 us: body(): noise_weight = inverse_var.reshape(row_count, wave_count) * usable]
where the time goes in v1:
time: 79.8 us; the launch traced here: 79.4 us
  blocking collectives  54.2 us (68%)
  Pallas kernels  11.3 us (14%)
  local copies, waits for them, and re-layouts  8.03 us (10%)
  starting transfers between devices  4.34 us (5%)
  waiting for transfers between devices  0.83 us (1%)
    all_to_all x1, blocking collectives, body(): lax.all_to_all(packed, 'fiber', 0, 0, axis_index_groups=near, tiled=True)  27.3 us
    all_to_all x1, blocking collectives, body(): lax.all_to_all(copies, 'fiber', 0, 0, axis_index_groups=far, tiled=True)  15.1 us
    all_to_all x1, blocking collectives, body(): lax.all_to_all(solved, 'fiber', 0, 0, axis_index_groups=near, tiled=True)  11.7 us
    unnamed x22, local copies, waits for them, and re-layouts  8.03 us
    pallas_call x1, Pallas kernels, body(): pl.pallas_call(residual_kernel, grid=(steps,), in_specs=[vmem(2 * fibers,...  5.35 us
    pallas_call x1, Pallas kernels, body(): pl.pallas_call(moments_kernel, grid=(steps,), in_specs=[pl.BlockSpec(memo...  4.83 us
    ppermute x1, starting transfers between devices, body(): lax.ppermute(chi_local, 'wave', [(h, (h + 1) % halves) for h in range(hal...  4.34 us
  transfers between devices with their start and end apart: 1, of which 1 were waited for; matrix products, arithmetic and copies ran while one was open for 0% of the time, Pallas kernels for 0%

profile of v1, /device:TPU:1, one launch (start us, length us, event | category | flops | bytes accessed | tf_op | source)
XLA Modules:
  0.0 79.4 jit_solution(15099607778648743202)
XLA Ops:
  0.6 0.0 copy-start
  0.6 1.7 %copy-done = f32[4,40,4096]{2,1,0:T(8,128)S(1)} copy-done((f32[4,40,4096]{2,1,0:T(8,128)S(1)}, f32[4,40,4096]{2,1,0:T(8,128)}, u32[]{:S(2)}) %copy-start) | copy-done | bytes 2621464
  2.4 0.0 copy-start.2
  2.4 1.7 %copy-done.2 = f32[4,40,4096]{2,1,0:T(8,128)S(1)} copy-done((f32[4,40,4096]{2,1,0:T(8,128)S(1)}, f32[4,40,4096]{2,1,0:T(8,128)}, u32[]{:S(2)}) %copy-start.2) | copy-done | bytes 2621464
  4.1 0.0 copy-start.4
  4.1 1.7 %copy-done.4 = s32[4,40,4096]{2,1,0:T(8,128)S(1)} copy-done((s32[4,40,4096]{2,1,0:T(8,128)S(1)}, s32[4,40,4096]{2,1,0:T(8,128)}, u32[]{:S(2)}) %copy-start.4) | copy-done | bytes 2621464
  5.9 0.0 copy-start.7
  5.9 0.8 copy-done.7
  6.6 0.0 copy-start.8
  6.6 0.7 copy-done.8
  7.3 0.0 copy-start.9
  7.3 0.7 copy-done.9
  8.0 0.0 copy-start.10
  8.0 0.7 copy-done.10
  8.7 0.0 copy-start.3
  8.7 0.0 copy-start.5
  8.7 4.8 %moments.1 = (f32[32,72,128]{2,1,0:T(8,128)S(1)}, f32[80,128]{1,0:T(8,128)S(1)}) custom-call(s32[40]{0:T(128)S(1)} %copy-done.10, f32[2,5120]{1,0:T(2,128)S(1)} %copy-done.7, f32[4,40]{1,0:T(4,128)S(1)} %copy-done.8, s32[4,40]{1,0:T(4,128)S(1)} %copy-done.9, f32[4,40,4096]{2,1,0:T(8,128)S(1)} %copy-done, f32[4,40,4096]{2,1,0:T(8,128)S(1)} %copy-done.2, ...), custom_call_target="tpu_custom_call" | custom-call | flops 283115520 | bytes 7864320 | tf_op jit(solution)/shard_map/moments/pallas_call | solution.py:260
  13.5 0.0 copy-start.6
  13.5 0.0 copy-start.1
  13.5 27.3 %all_to_all.15.in_ref = f32[32,72,128]{2,1,0:T(8,128)S(1)} all-to-all(f32[32,72,128]{2,1,0:T(8,128)S(1)} %get-tuple-element.9), channel_id=1, replica_groups={{0,2,4,6,8,10,12,14,16,18,20,22,24,26,28,30,32,34,36,38,40,42,44,46,48,..., dimensions={0} | all-to-all | bytes 2359296 | tf_op jit(solution)/shard_map/all_to_all | solution.py:288
  40.8 0.1 add.1
  40.9 15.1 %all_to_all.16.in_ref = f32[4,72,128]{2,1,0:T(8,128)S(1)} all-to-all(f32[4,72,128]{2,1,0:T(8,128)S(1)} %add.1), channel_id=1, replica_groups={{0,64,128,192},{2,66,130,194},{4,68,132,196},{6,70,134,198},{8,72,136,2..., dimensions={0} | all-to-all | bytes 294912 | tf_op jit(solution)/shard_map/all_to_all | solution.py:295
  56.0 0.0 copy-done.6
  56.0 0.4 solve.1
  56.5 11.7 %all_to_all.17.coeff_ref = f32[32,16,128]{2,1,0:T(8,128)S(1)} all-to-all(f32[32,16,128]{2,1,0:T(8,128)S(1)} %solve.1), channel_id=1, replica_groups={{0,2,4,6,8,10,12,14,16,18,20,22,24,26,28,30,32,34,36,38,40,42,44,46,48,..., dimensions={0} | all-to-all | bytes 524288 | tf_op jit(solution)/shard_map/all_to_all | solution.py:302
  68.2 0.0 copy-done.3
  68.2 0.0 copy-done.5
  68.2 0.0 copy-done.1
  68.2 5.3 %residual.1 = (f32[4,40,4096]{2,1,0:T(8,128)}, f32[16,4096]{1,0:T(8,128)}, f32[8,160]{1,0:T(8,128)S(1)}) custom-call(f32[80,128]{1,0:T(8,128)S(1)} %get-tuple-element.8.feat_ref, f32[32,16,128]{2,1,0:T(8,128)S(1)} %all_to_all.17.coeff_ref, f32[4,40,4096]{2,1,0:T(8,128)S(1)} %copy-done.1, f32[4,40,4096]{2,1,0:T(8,128)S(1)} %copy-done.3, ...), custom_call_target="tpu_custom_call" | custom-call | flops 31457280 | bytes 10485760 | tf_op jit(solution)/shard_map/residual/pallas_call | solution.py:304
  73.6 4.3 %collective-permute-start = (f32[8,160]{1,0:T(8,128)S(1)}, f32[8,160]{1,0:T(8,128)S(1)}, u32[]{:S(2)}, u32[]{:S(2)}) collective-permute-start(f32[8,160]{1,0:T(8,128)S(1)} %get-tuple-element.11.mine_ref), channel_id=1, source_target_pairs={{0,1},{1,0},{2,3},{3,2},{4,5},{5,4},{6,7},{7,6},{8,9},{9,8},{10,11... | collective-permute-start | bytes 15368 | tf_op jit(solution)/shard_map/ppermute | solution.py:329
  77.9 0.8 %collective-permute-done.other_ref = f32[8,160]{1,0:T(8,128)S(1)} collective-permute-done((f32[8,160]{1,0:T(8,128)S(1)}, f32[8,160]{1,0:T(8,128)S(1)}, u32[]{:S(2)}, u32[]{:S(2)}) %collective-permute-start) | collective-permute-done | bytes 5152 | tf_op jit(solution)/shard_map/ppermute | solution.py:329
  78.7 0.7 chi.1
Async XLA Ops:
  0.6 1.7 %copy-start = (f32[4,40,4096]{2,1,0:T(8,128)S(1)}, f32[4,40,4096]{2,1,0:T(8,128)}, u32[]{:S(2)}) copy-start(f32[4,40,4096]{2,1,0:T(8,128)} %flux_ref.3) | copy-start | bytes 7864324
  2.4 1.7 %copy-start.2 = (f32[4,40,4096]{2,1,0:T(8,128)S(1)}, f32[4,40,4096]{2,1,0:T(8,128)}, u32[]{:S(2)}) copy-start(f32[4,40,4096]{2,1,0:T(8,128)} %ivar_ref.3) | copy-start | bytes 7864324
  4.1 1.7 %copy-start.4 = (s32[4,40,4096]{2,1,0:T(8,128)S(1)}, s32[4,40,4096]{2,1,0:T(8,128)}, u32[]{:S(2)}) copy-start(s32[4,40,4096]{2,1,0:T(8,128)} %bits_ref.3) | copy-start | bytes 7864324
  5.9 0.8 copy-start.7
  6.6 0.7 copy-start.8
  7.3 0.7 copy-start.9
  8.0 0.7 copy-start.10
  8.7 59.5 %copy-start.3 = (f32[4,40,4096]{2,1,0:T(8,128)S(1)}, f32[4,40,4096]{2,1,0:T(8,128)}, u32[]{:S(2)}) copy-start(f32[4,40,4096]{2,1,0:T(8,128)} %ivar_ref.3) | copy-start | bytes 7864324
  8.7 59.5 %copy-start.5 = (s32[4,40,4096]{2,1,0:T(8,128)S(1)}, s32[4,40,4096]{2,1,0:T(8,128)}, u32[]{:S(2)}) copy-start(s32[4,40,4096]{2,1,0:T(8,128)} %bits_ref.3) | copy-start | bytes 7864324
  13.5 42.5 %copy-start.6 = (f32[256,128]{1,0:T(8,128)S(1)}, f32[256,128]{1,0:T(8,128)}, u32[]{:S(2)}) copy-start(f32[256,128]{1,0:T(8,128)} %constant.2.clone.table_ref) | copy-start | bytes 393220
  13.5 54.7 %copy-start.1 = (f32[4,40,4096]{2,1,0:T(8,128)S(1)}, f32[4,40,4096]{2,1,0:T(8,128)}, u32[]{:S(2)}) copy-start(f32[4,40,4096]{2,1,0:T(8,128)} %flux_ref.3) | copy-start | bytes 7864324
  73.6 5.2 %collective-permute-start = (f32[8,160]{1,0:T(8,128)S(1)}, f32[8,160]{1,0:T(8,128)S(1)}, u32[]{:S(2)}, u32[]{:S(2)}) collective-permute-start(f32[8,160]{1,0:T(8,128)S(1)} %get-tuple-element.11.mine_ref), channel_id=1, source_target_pairs={{0,1},{1,0},{2,3},{3,2},{4,5},{5,4},{6,7},{7,6},{8,9},{9,8},{10,11... | collective-permute-start | bytes 15368 | tf_op jit(solution)/shard_map/ppermute | solution.py:329

commit v2 on v1

v2 whole, which is shorter than its diff:
```python
import functools

import jax
import jax.numpy as jnp
from jax import lax
from jax.experimental import pallas as pl
from jax.experimental.pallas import tpu as pltpu
from jax.sharding import PartitionSpec as P

PARAMS = 16
BAD_BITS = 31
PRIOR = 1.0
MOMENTS = 7
BASIS = 4
RIGHT_ROW = 56
PACKED = 72
LANES = 128
PIECE = 512
FLOPS = 4_000_000_000


def legendre_series(coord, total):
    series = [jnp.ones_like(coord), coord]
    for order in range(1, total - 1):
        series.append(((2 * order + 1) * coord * series[order] - order * series[order - 1]) / (order + 1))
    return series


def monomial_table(total):
    coeffs = [[0.0] * total for _ in range(total)]
    coeffs[0][0] = 1.0
    coeffs[1][1] = 1.0
    for order in range(1, total - 1):
        for power in range(total):
            raised = coeffs[order][power - 1] if power >= 1 else 0.0
            coeffs[order + 1][power] = ((2 * order + 1) * raised - order * coeffs[order - 1][power]) / (order + 1)
    return coeffs


def product_series(higher, first, second):
    product = [0.0] * MOMENTS
    for left in range(MOMENTS):
        for right in range(MOMENTS - left):
            product[left + right] += higher[first][left] * higher[second][right]
    series = [0.0] * MOMENTS
    for order in reversed(range(MOMENTS)):
        now = product[order] / higher[order][order]
        series[order] = now
        for power in range(MOMENTS):
            product[power] -= now * higher[order][power]
    return series


def rebuild_rows():
    higher = monomial_table(MOMENTS)
    pair = [[product_series(higher, a, b) for b in range(BASIS)] for a in range(BASIS)]
    rows = []
    for i in range(BASIS):
        for j in range(BASIS):
            for k in range(BASIS):
                for l in range(BASIS):
                    row = [0.0] * LANES
                    for a in range(MOMENTS):
                        for b in range(MOMENTS):
                            row[a * MOMENTS + b] = pair[i][k][a] * pair[j][l][b]
                    rows.append(row)
    return rows


def split3(value):
    high = value.astype(jnp.bfloat16)
    rest = value - high.astype(jnp.float32)
    middle = rest.astype(jnp.bfloat16)
    low = (rest - middle.astype(jnp.float32)).astype(jnp.bfloat16)
    return high, middle, low


def dot6(left, right):
    l1, l2, l3 = split3(left)
    r1, r2, r3 = split3(right)
    total = None
    for a, b in ((l1, r3), (l3, r1), (l2, r2), (l1, r2), (l2, r1), (l1, r1)):
        part = jnp.dot(a, b, preferred_element_type=jnp.float32)
        total = part if total is None else total + part
    return total


def build_features(ids_ref, pos_ref, tput_ref, sky_ref, stack_ref, feat_ref, left_ref):
    exposures, fibers = tput_ref.shape
    stack_ref[0:LANES, :] = jnp.zeros((LANES, LANES), jnp.float32)
    stack_ref[0:exposures, 0:fibers] = tput_ref[...]
    stack_ref[8:8 + exposures, 0:fibers] = sky_ref[...].astype(jnp.float32)
    stack_ref[16:17, 0:fibers] = ids_ref[...].reshape(1, fibers).astype(jnp.float32)
    turned = stack_ref[0:LANES, :].T
    lane = lax.broadcasted_iota(jnp.int32, (fibers, LANES), 1)
    ids = jnp.broadcast_to(turned[0:fibers, 16:17], (fibers, LANES)).astype(jnp.int32)
    sum_x = jnp.zeros((fibers, LANES), jnp.float32)
    sum_y = jnp.zeros((fibers, LANES), jnp.float32)
    offset = ids - lane
    for tile in range(pos_ref.shape[1] // LANES):
        hit = offset == tile * LANES
        cut = slice(tile * LANES, (tile + 1) * LANES)
        sum_x = jnp.where(hit, pos_ref[0:1, cut], sum_x)
        sum_y = jnp.where(hit, pos_ref[1:2, cut], sum_y)
    coord_x = jnp.sum(sum_x, axis=1, keepdims=True)
    coord_y = jnp.sum(sum_y, axis=1, keepdims=True)
    series_x = legendre_series(jnp.broadcast_to(coord_x, (fibers, LANES)), MOMENTS)
    series_y = legendre_series(jnp.broadcast_to(coord_y, (fibers, LANES)), MOMENTS)
    is_right = lane >= RIGHT_ROW
    index_x = jnp.where(is_right, (lane - RIGHT_ROW) // BASIS, lane // MOMENTS)
    index_y = jnp.where(is_right, (lane - RIGHT_ROW) % BASIS, lane % MOMENTS)
    along_x = jnp.zeros((fibers, LANES), jnp.float32)
    along_y = jnp.zeros((fibers, LANES), jnp.float32)
    for order in range(MOMENTS):
        along_x = jnp.where(index_x == order, series_x[order], along_x)
        along_y = jnp.where(index_y == order, series_y[order], along_y)
    product = along_x * along_y
    moment_part = jnp.where(lane < MOMENTS * MOMENTS, product, 0.0)
    right_part = jnp.where(is_right & (lane < RIGHT_ROW + PARAMS), product, 0.0)
    feat_ref[0:fibers, :] = right_part
    feat_ref[fibers:2 * fibers, :] = turned[0:fibers, :]
    both = jnp.concatenate([moment_part, right_part], axis=0)
    high, middle, low = (part.astype(jnp.float32) for part in split3(both))
    rows = 2 * fibers
    for place, part in enumerate((high, middle, low, high, middle, high)):
        stack_ref[place * rows:(place + 1) * rows, :] = part
    stack_ref[6 * rows:, :] = jnp.zeros((stack_ref.shape[0] - 6 * rows, LANES), jnp.float32)
    for tile in range(stack_ref.shape[0] // LANES):
        cut = slice(tile * LANES, (tile + 1) * LANES)
        left_ref[:, cut] = stack_ref[cut, :].T[0:left_ref.shape[0], :].astype(jnp.bfloat16)


def piece_copies(flux_hbm, ivar_hbm, bits_hbm, flux_ref, ivar_ref, bits_ref, sems):
    copies = []
    for piece in range(flux_ref.shape[2] // PIECE):
        cut = pl.ds(piece * PIECE, PIECE)
        copies.append([
            pltpu.make_async_copy(source.at[:, :, cut], target.at[:, :, cut], sems.at[piece, which])
            for which, (source, target) in enumerate(((flux_hbm, flux_ref), (ivar_hbm, ivar_ref), (bits_hbm, bits_ref)))
        ])
    return copies


def sum_pieces(copies, feat_ref, left_ref, flux_ref, ivar_ref, bits_ref, out_ref, weight_ref):
    exposures, fibers, _ = flux_ref.shape
    columns = feat_ref[fibers:2 * fibers, :]
    for piece, trio in enumerate(copies):
        for copy in trio:
            copy.wait()
        here = slice(piece * PIECE, (piece + 1) * PIECE)
        moment_rows = None
        right_rows = None
        for e in range(exposures):
            through = columns[:, e:e + 1]
            sky = columns[:, 8 + e:9 + e]
            weight = jnp.where((bits_ref[e, :, here] & BAD_BITS) == 0, ivar_ref[e, :, here], 0.0)
            weight_ref[e, :, here] = weight
            first = weight * (through * sky)
            a = first * through
            b = first * flux_ref[e, :, here]
            moment_rows = a if e == 0 else moment_rows + a
            right_rows = b if e == 0 else right_rows + b
        high, middle, low = split3(jnp.concatenate([moment_rows, right_rows], axis=0))
        right = jnp.concatenate([high, high, high, middle, middle, low], axis=0)
        sums = jnp.dot(left_ref[:, 0:right.shape[0]], right, preferred_element_type=jnp.float32)
        for k in range(PIECE // LANES):
            out_ref[piece * (PIECE // LANES) + k] = sums[0:PACKED, k * LANES:(k + 1) * LANES]


def moments_kernel(ids_hbm, pos_hbm, tput_hbm, sky_hbm, flux_hbm, ivar_hbm, bits_hbm, out_ref, feat_ref, flux_ref, weight_ref,
                   ids_ref, pos_ref, tput_ref, sky_ref, ivar_ref, bits_ref, left_ref, stack_ref, small_sems, sems):
    small = [
        pltpu.make_async_copy(source, target, small_sems.at[place])
        for place, (source, target) in enumerate(((ids_hbm, ids_ref), (pos_hbm, pos_ref), (tput_hbm, tput_ref), (sky_hbm, sky_ref)))
    ]
    for copy in small:
        copy.start()
    copies = piece_copies(flux_hbm, ivar_hbm, bits_hbm, flux_ref, ivar_ref, bits_ref, sems)
    for trio in copies:
        for copy in trio:
            copy.start()
    for copy in small:
        copy.wait()
    build_features(ids_ref, pos_ref, tput_ref, sky_ref, stack_ref, feat_ref, left_ref)
    sum_pieces(copies, feat_ref, left_ref, flux_ref, ivar_ref, bits_ref, out_ref, weight_ref)


def add_kernel(in_ref, out_ref):
    total = in_ref[0]
    for source in range(1, in_ref.shape[0]):
        total = total + in_ref[source]
    for target in range(out_ref.shape[0]):
        out_ref[target] = total


def solve_kernel(in_ref, table_ref, out_ref):
    total = in_ref[0]
    for source in range(1, in_ref.shape[0]):
        total = total + in_ref[source]
    moments = jnp.concatenate([total[0:RIGHT_ROW], jnp.zeros((LANES - RIGHT_ROW, LANES), jnp.float32)], axis=0)
    normal = dot6(table_ref[...], moments)
    sub = lax.broadcasted_iota(jnp.int32, (PARAMS, LANES), 0)
    columns = []
    for k in range(PARAMS):
        column = normal[k * PARAMS:(k + 1) * PARAMS]
        columns.append(jnp.where(sub == k, column + PRIOR, column))
    right = total[RIGHT_ROW:RIGHT_ROW + PARAMS]
    scale = jnp.zeros((PARAMS, LANES), jnp.float32)
    for j in range(PARAMS):
        inverse = 1.0 / columns[j][j:j + 1]
        scale = jnp.where(sub == j, inverse, scale)
        factor = jnp.where(sub == j, 0.0, columns[j] * inverse)
        for l in range(j + 1, PARAMS):
            columns[l] = columns[l] - factor * columns[l][j:j + 1]
        right = right - factor * right[j:j + 1]
    right = right * scale
    for target in range(out_ref.shape[0]):
        out_ref[target] = right


def joined(coeff_ref, first, count):
    return jnp.concatenate([coeff_ref[first + k] for k in range(count)], axis=1)


def chi_sum_kernel(feat_ref, coeff_ref, flux_ref, weight_ref, chi_ref, sum_ref):
    exposures, fibers, waves = flux_ref.shape
    basis = feat_ref[0:fibers, RIGHT_ROW:RIGHT_ROW + PARAMS]
    sums = [None] * exposures
    for piece in range(waves // PIECE):
        here = slice(piece * PIECE, (piece + 1) * PIECE)
        model = dot6(basis, joined(coeff_ref, piece * (PIECE // LANES), PIECE // LANES))
        for e in range(exposures):
            residual = flux_ref[e, :, here] - feat_ref[fibers:2 * fibers, e:e + 1] * model
            chi = weight_ref[e, :, here] * residual * residual
            for k in range(PIECE // LANES):
                part = chi[:, k * LANES:(k + 1) * LANES]
                sums[e] = part if sums[e] is None else sums[e] + part
    for e in range(exposures):
        sum_ref[e * fibers:(e + 1) * fibers, :] = sums[e]
    ones = jnp.ones((8, LANES), jnp.float32)
    chi_ref[...] = lax.dot_general(ones, sum_ref[...], (((1,), (1,)), ((), ())), precision=lax.Precision.HIGHEST, preferred_element_type=jnp.float32)


def write_kernel(feat_ref, coeff_ref, flux_ref, res_hbm, all_hbm, res_ref, all_ref, sems, all_sem):
    exposures, fibers, waves = flux_ref.shape
    basis = feat_ref[0:fibers, RIGHT_ROW:RIGHT_ROW + PARAMS]
    copies = []
    for piece in range(waves // PIECE):
        here = slice(piece * PIECE, (piece + 1) * PIECE)
        coeffs = joined(coeff_ref, piece * (PIECE // LANES), PIECE // LANES)
        all_ref[:, here] = coeffs
        model = dot6(basis, coeffs)
        for e in range(exposures):
            res_ref[e, :, here] = flux_ref[e, :, here] - feat_ref[fibers:2 * fibers, e:e + 1] * model
        cut = pl.ds(piece * PIECE, PIECE)
        copies.append(pltpu.make_async_copy(res_ref.at[:, :, cut], res_hbm.at[:, :, cut], sems.at[piece]))
        copies[-1].start()
    copies.append(pltpu.make_async_copy(all_ref, all_hbm, all_sem))
    copies[-1].start()
    for copy in copies:
        copy.wait()


def chi_kernel(scale, mine_ref, other_ref, out_ref):
    exposures, fibers = out_ref.shape
    total = (mine_ref[...] + other_ref[...]) * scale
    for e in range(exposures):
        out_ref[e:e + 1, :] = total[0:1, e * fibers:(e + 1) * fibers]


def cost(flops, moved):
    return pl.CostEstimate(flops=flops, bytes_accessed=moved, transcendentals=0)


def params(limit_mib, dims=0):
    semantics = {"dimension_semantics": ("arbitrary",) * dims} if dims else {}
    return pltpu.CompilerParams(vmem_limit_bytes=limit_mib * 1024 * 1024, **semantics)


def groups(sizes):
    nz, ny, nx = sizes

    def place(z, y, x):
        return (z * ny + y) * nx + x

    pair = 2
    near = [[place(q * pair + h, y, x) for h in range(pair) for y in range(ny) for x in range(nx)] for q in range(nz // pair)]
    far = [[place(q * pair + h, y, x) for q in range(nz // pair)] for h in range(pair) for y in range(ny) for x in range(nx)]
    return near, far


VMEM = pl.BlockSpec(memory_space=pltpu.VMEM)
HBM = pl.BlockSpec(memory_space=pltpu.HBM)


def make_body(near, far):
    def body(spectra, inverse_var, mask_bits, sky_flags, fiber_ids, positions, throughput):
        exposures, fibers, waves = spectra.shape
        f32 = jnp.float32
        pieces = waves // PIECE
        stacked = -(-12 * fibers // LANES) * LANES
        moved = 4 * exposures * fibers * waves

        held = [
            pltpu.with_memory_space_constraint(value, pltpu.HBM)
            for value in (fiber_ids, positions, throughput, sky_flags, spectra, inverse_var, mask_bits)
        ]
        packed, feats, flux, weight = pl.pallas_call(
            moments_kernel,
            in_specs=[HBM] * 7,
            out_specs=[VMEM] * 4,
            out_shape=[
                jax.ShapeDtypeStruct((waves // LANES, PACKED, LANES), f32),
                jax.ShapeDtypeStruct((2 * fibers, LANES), f32),
                jax.ShapeDtypeStruct(spectra.shape, f32),
                jax.ShapeDtypeStruct(spectra.shape, f32),
            ],
            scratch_shapes=[
                pltpu.VMEM(fiber_ids.shape, jnp.int32),
                pltpu.VMEM(positions.shape, f32),
                pltpu.VMEM((exposures, fibers), f32),
                pltpu.VMEM((exposures, fibers), jnp.int32),
                pltpu.VMEM(spectra.shape, f32),
                pltpu.VMEM(spectra.shape, jnp.int32),
                pltpu.VMEM((80, stacked), jnp.bfloat16),
                pltpu.VMEM((stacked, LANES), f32),
                pltpu.SemaphoreType.DMA((4,)),
                pltpu.SemaphoreType.DMA((pieces, 3)),
            ],
            compiler_params=params(20),
            cost_estimate=cost(FLOPS, 3 * moved),
            name="moments",
        )(*held)

        arrived = lax.all_to_all(packed, "fiber", 0, 0, axis_index_groups=near, tiled=True)
        copies = pl.pallas_call(
            add_kernel,
            out_shape=jax.ShapeDtypeStruct((len(far[0]), PACKED, LANES), f32),
            compiler_params=params(8),
            name="add",
        )(arrived)
        parts = lax.all_to_all(copies, "fiber", 0, 0, axis_index_groups=far, tiled=True)
        solved = pl.pallas_call(
            solve_kernel,
            out_shape=jax.ShapeDtypeStruct((len(near[0]), PARAMS, LANES), f32),
            compiler_params=params(8),
            name="solve",
        )(parts, jnp.asarray(rebuild_rows(), f32))
        coeffs = lax.all_to_all(solved, "fiber", 0, 0, axis_index_groups=near, tiled=True)

        chi_local = pl.pallas_call(
            chi_sum_kernel,
            in_specs=[VMEM] * 4,
            out_specs=VMEM,
            out_shape=jax.ShapeDtypeStruct((8, exposures * fibers), f32),
            scratch_shapes=[pltpu.VMEM((exposures * fibers, LANES), f32)],
            compiler_params=params(16),
            cost_estimate=cost(FLOPS // 2, 0),
            name="chisum",
        )(feats, coeffs, flux, weight)
        halves = lax.axis_size("wave")
        chi_other = lax.ppermute(chi_local, "wave", [(h, (h + 1) % halves) for h in range(halves)])
        residual, sky_coeffs = pl.pallas_call(
            write_kernel,
            in_specs=[VMEM] * 3,
            out_specs=[HBM] * 2,
            out_shape=[
                jax.ShapeDtypeStruct(spectra.shape, f32),
                jax.ShapeDtypeStruct((PARAMS, waves), f32),
            ],
            scratch_shapes=[
                pltpu.VMEM(spectra.shape, f32),
                pltpu.VMEM((PARAMS, waves), f32),
                pltpu.SemaphoreType.DMA((pieces,)),
                pltpu.SemaphoreType.DMA,
            ],
            compiler_params=params(16),
            cost_estimate=cost(FLOPS, moved),
            name="residual",
        )(feats, coeffs, flux)
        chi_square = pl.pallas_call(
            functools.partial(chi_kernel, 1.0 / (waves * halves)),
            out_shape=jax.ShapeDtypeStruct((exposures, fibers), f32),
            compiler_params=params(4),
            name="chi",
        )(chi_local, chi_other)
        return residual, chi_square, sky_coeffs

    return body


def solution(mesh):
    near, far = groups((8, 4, 4))
    placed = (
        P(None, "fiber", "wave"),
        P(None, "fiber", "wave"),
        P(None, "fiber", "wave"),
        P(None, "fiber"),
        P("fiber"),
        P(),
        P(None, "fiber"),
    )
    return jax.shard_map(
        make_body(near, far),
        mesh=mesh,
        in_specs=placed,
        out_specs=(P(None, "fiber", "wave"), P(None, "fiber"), P(None, "wave")),
        check_vma=False,
    )
```

time: 79.8 us -> 69.8 us (0.87)
  local copies, waits for them, and re-layouts: 8.03 us -> 0.01 us
  waiting for transfers between devices: 0.83 us -> 0.01 us
  Pallas kernels: 11.3 us -> 10.5 us
    unnamed x22 -> x2, local copies, waits for them, and re-layouts: 8.03 us -> 0.01 us
    ppermute x1, waiting for transfers between devices: 0.83 us -> 0.01 us  [body(): lax.ppermute(chi_local, 'wave', [(h, (h + 1) % halves) for h in range(hal...]
    pallas_call x2 -> x3, Pallas kernels: 10.2 us -> 9.36 us  [the longest x1 6.24 us: body(): pl.pallas_call(moments_kernel, in_specs=[HBM] * 7, out_specs=[VMEM] * 4,...]
  transfers between devices with their start and end apart: 1 -> 1, of which waited for: 1 -> 0; matrix products, arithmetic and copies ran while one was open for 0% -> 0% of each run, Pallas kernels for 0% -> 3%
where the time goes in v2:
time: 69.8 us; the launch traced here: 69.6 us
  blocking collectives  54 us (77%)
  Pallas kernels  10.5 us (15%)
  starting transfers between devices  4.34 us (6%)
    all_to_all x1, blocking collectives, body(): lax.all_to_all(packed, 'fiber', 0, 0, axis_index_groups=near, tiled=True)  27.2 us
    all_to_all x1, blocking collectives, body(): lax.all_to_all(copies, 'fiber', 0, 0, axis_index_groups=far, tiled=True)  15.1 us
    all_to_all x1, blocking collectives, body(): lax.all_to_all(solved, 'fiber', 0, 0, axis_index_groups=near, tiled=True)  11.7 us
    pallas_call x1, Pallas kernels, body(): pl.pallas_call(moments_kernel, in_specs=[HBM] * 7, out_specs=[VMEM] * 4,...  6.24 us
    ppermute x1, starting transfers between devices, body(): lax.ppermute(chi_local, 'wave', [(h, (h + 1) % halves) for h in range(hal...  4.34 us
    pallas_call x1, Pallas kernels, body(): pl.pallas_call(write_kernel, in_specs=[VMEM] * 3, out_specs=[HBM] * 2, ou...  1.95 us
  transfers between devices with their start and end apart: 1, of which 0 were waited for; matrix products, arithmetic and copies ran while one was open for 0% of the time, Pallas kernels for 3%

profile of v2, /device:TPU:1, one launch (start us, length us, event | category | flops | bytes accessed | tf_op | source)
XLA Modules:
  0.0 69.6 jit_solution(16234062203182531613)
XLA Ops:
  0.6 6.2 %moments.1 = (f32[32,72,128]{2,1,0:T(8,128)S(1)}, f32[80,128]{1,0:T(8,128)S(1)}, f32[4,40,4096]{2,1,0:T(8,128)S(1)}, f32[4,40,4096]{2,1,0:T(8,128)S(1)}) custom-call(s32[40]{0:T(128)} %ids_hbm.1, f32[2,5120]{1,0:T(2,128)} %pos_hbm.1, f32[4,40]{1,0:T(4,128)} %tput_hbm.1, s32[4,40]{1,0:T(4,128)} %sky_hbm.1, f32[4,40,4096]{2,1,0:T(8,128)} %flux_hbm.1, ...), custom_call_target="tpu_custom_call" | custom-call | flops 4000000000 | bytes 7864320 | tf_op jit(solution)/shard_map/moments/pallas_call | solution.py:308
  6.9 0.0 copy-start
  6.9 27.2 %all_to_all.15.in_ref = f32[32,72,128]{2,1,0:T(8,128)S(1)} all-to-all(f32[32,72,128]{2,1,0:T(8,128)S(1)} %get-tuple-element.10), channel_id=1, replica_groups={{0,2,4,6,8,10,12,14,16,18,20,22,24,26,28,30,32,34,36,38,40,42,44,46,48,..., dimensions={0} | all-to-all | bytes 2359296 | tf_op jit(solution)/shard_map/all_to_all | solution.py:335
  34.1 0.1 add.1
  34.1 15.1 %all_to_all.16.in_ref = f32[4,72,128]{2,1,0:T(8,128)S(1)} all-to-all(f32[4,72,128]{2,1,0:T(8,128)S(1)} %add.1), channel_id=1, replica_groups={{0,64,128,192},{2,66,130,194},{4,68,132,196},{6,70,134,198},{8,72,136,2..., dimensions={0} | all-to-all | bytes 294912 | tf_op jit(solution)/shard_map/all_to_all | solution.py:342
  49.3 0.0 copy-done
  49.3 0.4 solve.1
  49.7 11.7 %all_to_all.17.coeff_ref = f32[32,16,128]{2,1,0:T(8,128)S(1)} all-to-all(f32[32,16,128]{2,1,0:T(8,128)S(1)} %solve.1), channel_id=1, replica_groups={{0,2,4,6,8,10,12,14,16,18,20,22,24,26,28,30,32,34,36,38,40,42,44,46,48,..., dimensions={0} | all-to-all | bytes 524288 | tf_op jit(solution)/shard_map/all_to_all | solution.py:349
  61.4 1.2 %chisum.1.mine_ref = f32[8,160]{1,0:T(8,128)S(1)} custom-call(f32[80,128]{1,0:T(8,128)S(1)} %get-tuple-element.9.feat_ref, f32[32,16,128]{2,1,0:T(8,128)S(1)} %all_to_all.17.coeff_ref, f32[4,40,4096]{2,1,0:T(8,128)S(1)} %get-tuple-element.11.flux_ref, f32[4,40,4096]{2,1,0:T(8,128)S(1)} %get-tuple-element.13.weight_ref), custom_call_target="tpu_custom_call" | custom-call | flops 2000000000 | tf_op jit(solution)/shard_map/chisum/pallas_call | solution.py:351
  62.6 4.3 %collective-permute-start = (f32[8,160]{1,0:T(8,128)S(1)}, f32[8,160]{1,0:T(8,128)S(1)}, u32[]{:S(2)}, u32[]{:S(2)}) collective-permute-start(f32[8,160]{1,0:T(8,128)S(1)} %chisum.1.mine_ref), channel_id=1, source_target_pairs={{0,1},{1,0},{2,3},{3,2},{4,5},{5,4},{6,7},{7,6},{8,9},{9,8},{10,11... | collective-permute-start | bytes 15368 | tf_op jit(solution)/shard_map/ppermute | solution.py:362
  67.0 1.9 %residual.1 = (f32[4,40,4096]{2,1,0:T(8,128)}, f32[16,4096]{1,0:T(8,128)}) custom-call(f32[80,128]{1,0:T(8,128)S(1)} %get-tuple-element.9.feat_ref, f32[32,16,128]{2,1,0:T(8,128)S(1)} %all_to_all.17.coeff_ref, f32[4,40,4096]{2,1,0:T(8,128)S(1)} %get-tuple-element.11.flux_ref), custom_call_target="tpu_custom_call" | custom-call | flops 4000000000 | bytes 2621440 | tf_op jit(solution)/shard_map/residual/pallas_call | solution.py:363
  68.9 0.0 collective-permute-done.other_ref
  68.9 0.7 chi.1
Async XLA Ops:
  6.9 42.4 %copy-start = (f32[256,128]{1,0:T(8,128)S(1)}, f32[256,128]{1,0:T(8,128)}, u32[]{:S(2)}) copy-start(f32[256,128]{1,0:T(8,128)} %constant.2.clone.table_ref) | copy-start | bytes 393220
  62.6 6.3 %collective-permute-start = (f32[8,160]{1,0:T(8,128)S(1)}, f32[8,160]{1,0:T(8,128)S(1)}, u32[]{:S(2)}, u32[]{:S(2)}) collective-permute-start(f32[8,160]{1,0:T(8,128)S(1)} %chisum.1.mine_ref), channel_id=1, source_target_pairs={{0,1},{1,0},{2,3},{3,2},{4,5},{5,4},{6,7},{7,6},{8,9},{9,8},{10,11... | collective-permute-start | bytes 15368 | tf_op jit(solution)/shard_map/ppermute | solution.py:362

commit v3 on v2

--- a/solution.py
+++ b/solution.py
@@ -15,7 +15,11 @@
 RIGHT_ROW = 56
 PACKED = 72
 LANES = 128
+PAIR = 1
 PIECE = 512
+WRITE = 1024
+EARLY = 2048
+GRAIN = 2048
 FLOPS = 4_000_000_000
 
 
@@ -132,8 +136,8 @@
 
 def piece_copies(flux_hbm, ivar_hbm, bits_hbm, flux_ref, ivar_ref, bits_ref, sems):
     copies = []
-    for piece in range(flux_ref.shape[2] // PIECE):
-        cut = pl.ds(piece * PIECE, PIECE)
+    for piece in range(flux_ref.shape[2] // GRAIN):
+        cut = pl.ds(piece * GRAIN, GRAIN)
         copies.append([
             pltpu.make_async_copy(source.at[:, :, cut], target.at[:, :, cut], sems.at[piece, which])
             for which, (source, target) in enumerate(((flux_hbm, flux_ref), (ivar_hbm, ivar_ref), (bits_hbm, bits_ref)))
@@ -144,9 +148,10 @@
 def sum_pieces(copies, feat_ref, left_ref, flux_ref, ivar_ref, bits_ref, out_ref, weight_ref):
     exposures, fibers, _ = flux_ref.shape
     columns = feat_ref[fibers:2 * fibers, :]
-    for piece, trio in enumerate(copies):
-        for copy in trio:
-            copy.wait()
+    for piece in range(flux_ref.shape[2] // PIECE):
+        if piece * PIECE % GRAIN == 0:
+            for copy in copies[piece * PIECE // GRAIN]:
+                copy.wait()
         here = slice(piece * PIECE, (piece + 1) * PIECE)
         moment_rows = None
         right_rows = None
@@ -176,9 +181,9 @@
     for copy in small:
         copy.start()
     copies = piece_copies(flux_hbm, ivar_hbm, bits_hbm, flux_ref, ivar_ref, bits_ref, sems)
-    for trio in copies:
-        for copy in trio:
-            copy.start()
+    for place, trio in enumerate(copies):
+        for which, copy in enumerate(trio):
+            copy.start(priority=(place + which) % 2)
     for copy in small:
         copy.wait()
     build_features(ids_ref, pos_ref, tput_ref, sky_ref, stack_ref, feat_ref, left_ref)
@@ -193,12 +198,9 @@
         out_ref[target] = total
 
 
-def solve_kernel(in_ref, table_ref, out_ref):
-    total = in_ref[0]
-    for source in range(1, in_ref.shape[0]):
-        total = total + in_ref[source]
+def solve_one(total, table):
     moments = jnp.concatenate([total[0:RIGHT_ROW], jnp.zeros((LANES - RIGHT_ROW, LANES), jnp.float32)], axis=0)
-    normal = dot6(table_ref[...], moments)
+    normal = dot6(table, moments)
     sub = lax.broadcasted_iota(jnp.int32, (PARAMS, LANES), 0)
     columns = []
     for k in range(PARAMS):
@@ -213,17 +215,31 @@
         for l in range(j + 1, PARAMS):
             columns[l] = columns[l] - factor * columns[l][j:j + 1]
         right = right - factor * right[j:j + 1]
-    right = right * scale
+    return right * scale
+
+
+def solve_kernel(in_ref, table_ref, out_ref):
+    total = in_ref[0]
+    for source in range(1, in_ref.shape[0]):
+        total = total + in_ref[source]
+    table = table_ref[...]
+    stretches = in_ref.shape[1] // PACKED
+    solved = jnp.concatenate([solve_one(total[t * PACKED:(t + 1) * PACKED], table) for t in range(stretches)], axis=0)
     for target in range(out_ref.shape[0]):
-        out_ref[target] = right
+        out_ref[target] = solved
 
 
 def joined(coeff_ref, first, count):
     return jnp.concatenate([coeff_ref[first + k] for k in range(count)], axis=1)
 
 
-def chi_sum_kernel(feat_ref, coeff_ref, flux_ref, weight_ref, chi_ref, sum_ref):
+def residual_kernel(feat_ref, coeff_ref, flux_ref, weight_ref, chi_ref, late_ref, res_hbm, all_hbm, sum_ref, early_ref, all_ref, sems, all_sem):
     exposures, fibers, waves = flux_ref.shape
+    chunks = waves // LANES
+    early = early_ref.shape[2]
+    all_ref[...] = joined(coeff_ref, 0, chunks)
+    copies = [pltpu.make_async_copy(all_ref, all_hbm, all_sem)]
+    copies[0].start(priority=1)
     basis = feat_ref[0:fibers, RIGHT_ROW:RIGHT_ROW + PARAMS]
     sums = [None] * exposures
     for piece in range(waves // PIECE):
@@ -231,32 +247,36 @@
         model = dot6(basis, joined(coeff_ref, piece * (PIECE // LANES), PIECE // LANES))
         for e in range(exposures):
             residual = flux_ref[e, :, here] - feat_ref[fibers:2 * fibers, e:e + 1] * model
+            if piece * PIECE < early:
+                early_ref[e, :, here] = residual
+            else:
+                late_ref[e, :, piece * PIECE - early:(piece + 1) * PIECE - early] = residual
             chi = weight_ref[e, :, here] * residual * residual
             for k in range(PIECE // LANES):
                 part = chi[:, k * LANES:(k + 1) * LANES]
                 sums[e] = part if sums[e] is None else sums[e] + part
+        done = (piece + 1) * PIECE
+        if done <= early and done % WRITE == 0:
+            cut = pl.ds(done - WRITE, WRITE)
+            copies.append(pltpu.make_async_copy(early_ref.at[:, :, cut], res_hbm.at[:, :, cut], sems.at[done // WRITE - 1]))
+            copies[-1].start(priority=done // WRITE % 2)
     for e in range(exposures):
         sum_ref[e * fibers:(e + 1) * fibers, :] = sums[e]
     ones = jnp.ones((8, LANES), jnp.float32)
     chi_ref[...] = lax.dot_general(ones, sum_ref[...], (((1,), (1,)), ((), ())), precision=lax.Precision.HIGHEST, preferred_element_type=jnp.float32)
-
-
-def write_kernel(feat_ref, coeff_ref, flux_ref, res_hbm, all_hbm, res_ref, all_ref, sems, all_sem):
-    exposures, fibers, waves = flux_ref.shape
-    basis = feat_ref[0:fibers, RIGHT_ROW:RIGHT_ROW + PARAMS]
-    copies = []
-    for piece in range(waves // PIECE):
-        here = slice(piece * PIECE, (piece + 1) * PIECE)
-        coeffs = joined(coeff_ref, piece * (PIECE // LANES), PIECE // LANES)
-        all_ref[:, here] = coeffs
-        model = dot6(basis, coeffs)
-        for e in range(exposures):
-            res_ref[e, :, here] = flux_ref[e, :, here] - feat_ref[fibers:2 * fibers, e:e + 1] * model
-        cut = pl.ds(piece * PIECE, PIECE)
-        copies.append(pltpu.make_async_copy(res_ref.at[:, :, cut], res_hbm.at[:, :, cut], sems.at[piece]))
-        copies[-1].start()
-    copies.append(pltpu.make_async_copy(all_ref, all_hbm, all_sem))
-    copies[-1].start()
+    for copy in copies:
+        copy.wait()
+
+
+def late_kernel(late_ref, _, res_hbm, sems):
+    width = late_ref.shape[2]
+    begin = res_hbm.shape[2] - width
+    copies = [
+        pltpu.make_async_copy(late_ref.at[e], res_hbm.at[e, :, pl.ds(begin, width)], sems.at[e])
+        for e in range(late_ref.shape[0])
+    ]
+    for e, copy in enumerate(copies):
+        copy.start(priority=e % 2)
     for copy in copies:
         copy.wait()
 
@@ -283,7 +303,7 @@
     def place(z, y, x):
         return (z * ny + y) * nx + x
 
-    pair = 2
+    pair = PAIR
     near = [[place(q * pair + h, y, x) for h in range(pair) for y in range(ny) for x in range(nx)] for q in range(nz // pair)]
     far = [[place(q * pair + h, y, x) for q in range(nz // pair)] for h in range(pair) for y in range(ny) for x in range(nx)]
     return near, far
@@ -297,7 +317,6 @@
     def body(spectra, inverse_var, mask_bits, sky_flags, fiber_ids, positions, throughput):
         exposures, fibers, waves = spectra.shape
         f32 = jnp.float32
-        pieces = waves // PIECE
         stacked = -(-12 * fibers // LANES) * LANES
         moved = 4 * exposures * fibers * waves
 
@@ -325,59 +344,67 @@
                 pltpu.VMEM((80, stacked), jnp.bfloat16),
                 pltpu.VMEM((stacked, LANES), f32),
                 pltpu.SemaphoreType.DMA((4,)),
-                pltpu.SemaphoreType.DMA((pieces, 3)),
+                pltpu.SemaphoreType.DMA((waves // GRAIN, 3)),
             ],
             compiler_params=params(20),
             cost_estimate=cost(FLOPS, 3 * moved),
             name="moments",
         )(*held)
 
+        members = len(near[0])
+        rows = waves // LANES // members * PACKED
+        packed = packed.reshape(members, rows, LANES)
         arrived = lax.all_to_all(packed, "fiber", 0, 0, axis_index_groups=near, tiled=True)
         copies = pl.pallas_call(
             add_kernel,
-            out_shape=jax.ShapeDtypeStruct((len(far[0]), PACKED, LANES), f32),
+            out_shape=jax.ShapeDtypeStruct((len(far[0]), rows, LANES), f32),
             compiler_params=params(8),
             name="add",
         )(arrived)
         parts = lax.all_to_all(copies, "fiber", 0, 0, axis_index_groups=far, tiled=True)
         solved = pl.pallas_call(
             solve_kernel,
-            out_shape=jax.ShapeDtypeStruct((len(near[0]), PARAMS, LANES), f32),
+            out_shape=jax.ShapeDtypeStruct((members, rows // PACKED * PARAMS, LANES), f32),
             compiler_params=params(8),
             name="solve",
         )(parts, jnp.asarray(rebuild_rows(), f32))
         coeffs = lax.all_to_all(solved, "fiber", 0, 0, axis_index_groups=near, tiled=True)
-
-        chi_local = pl.pallas_call(
-            chi_sum_kernel,
+        coeffs = coeffs.reshape(waves // LANES, PARAMS, LANES)
+
+        chi_local, late, residual, sky_coeffs = pl.pallas_call(
+            residual_kernel,
             in_specs=[VMEM] * 4,
-            out_specs=VMEM,
-            out_shape=jax.ShapeDtypeStruct((8, exposures * fibers), f32),
-            scratch_shapes=[pltpu.VMEM((exposures * fibers, LANES), f32)],
-            compiler_params=params(16),
-            cost_estimate=cost(FLOPS // 2, 0),
-            name="chisum",
-        )(feats, coeffs, flux, weight)
-        halves = lax.axis_size("wave")
-        chi_other = lax.ppermute(chi_local, "wave", [(h, (h + 1) % halves) for h in range(halves)])
-        residual, sky_coeffs = pl.pallas_call(
-            write_kernel,
-            in_specs=[VMEM] * 3,
-            out_specs=[HBM] * 2,
+            out_specs=[VMEM, VMEM, HBM, HBM],
             out_shape=[
+                jax.ShapeDtypeStruct((8, exposures * fibers), f32),
+                jax.ShapeDtypeStruct((exposures, fibers, waves - EARLY), f32),
                 jax.ShapeDtypeStruct(spectra.shape, f32),
                 jax.ShapeDtypeStruct((PARAMS, waves), f32),
             ],
             scratch_shapes=[
-                pltpu.VMEM(spectra.shape, f32),
+                pltpu.VMEM((exposures * fibers, LANES), f32),
+                pltpu.VMEM((exposures, fibers, EARLY), f32),
                 pltpu.VMEM((PARAMS, waves), f32),
-                pltpu.SemaphoreType.DMA((pieces,)),
+                pltpu.SemaphoreType.DMA((EARLY // WRITE,)),
                 pltpu.SemaphoreType.DMA,
             ],
             compiler_params=params(16),
             cost_estimate=cost(FLOPS, moved),
             name="residual",
-        )(feats, coeffs, flux)
+        )(feats, coeffs, flux, weight)
+        halves = lax.axis_size("wave")
+        chi_other = lax.ppermute(chi_local, "wave", [(h, (h + 1) % halves) for h in range(halves)])
+        residual = pl.pallas_call(
+            late_kernel,
+            in_specs=[VMEM, HBM],
+            out_specs=HBM,
+            out_shape=jax.ShapeDtypeStruct(spectra.shape, f32),
+            input_output_aliases={1: 0},
+            scratch_shapes=[pltpu.SemaphoreType.DMA((exposures,))],
+            compiler_params=params(4),
+            cost_estimate=cost(FLOPS, moved),
+            name="late",
+        )(late, residual)
         chi_square = pl.pallas_call(
             functools.partial(chi_kernel, 1.0 / (waves * halves)),
             out_shape=jax.ShapeDtypeStruct((exposures, fibers), f32),

time: 69.8 us -> 74.5 us (1.067)
  blocking collectives: 54 us -> 59.4 us
  Pallas kernels: 10.5 us -> 8.63 us
  starting transfers between devices: 4.34 us -> 5.59 us
    all_to_all x1, blocking collectives: 15.1 us -> 23.7 us  [body(): lax.all_to_all(copies, 'fiber', 0, 0, axis_index_groups=far, tiled=True)]
    all_to_all x1, blocking collectives: 27.2 us -> 25 us  [body(): lax.all_to_all(packed, 'fiber', 0, 0, axis_index_groups=near, tiled=True)]
    pallas_call x1, Pallas kernels: 6.24 us -> 4.3 us  [body(): pl.pallas_call(moments_kernel, in_specs=[HBM] * 7, out_specs=[VMEM] * 4,...]
    ppermute x1, starting transfers between devices: 4.34 us -> 5.59 us  [body(): lax.ppermute(chi_local, 'wave', [(h, (h + 1) % halves) for h in range(hal...]
    all_to_all x1, blocking collectives: 11.7 us -> 10.7 us  [body(): lax.all_to_all(solved, 'fiber', 0, 0, axis_index_groups=near, tiled=True)]
  transfers between devices with their start and end apart: 1 -> 1, of which waited for: 0 -> 0; matrix products, arithmetic and copies ran while one was open for 0% -> 0% of each run, Pallas kernels for 3% -> 1%
where the time goes in v3:
time: 74.5 us; the launch traced here: 74.3 us
  blocking collectives  59.4 us (80%)
  Pallas kernels  8.63 us (12%)
  starting transfers between devices  5.59 us (8%)
    all_to_all x1, blocking collectives, body(): lax.all_to_all(packed, 'fiber', 0, 0, axis_index_groups=near, tiled=True)  25 us
    all_to_all x1, blocking collectives, body(): lax.all_to_all(copies, 'fiber', 0, 0, axis_index_groups=far, tiled=True)  23.7 us
    all_to_all x1, blocking collectives, body(): lax.all_to_all(solved, 'fiber', 0, 0, axis_index_groups=near, tiled=True)  10.7 us
    ppermute x1, starting transfers between devices, body(): lax.ppermute(chi_local, 'wave', [(h, (h + 1) % halves) for h in range(hal...  5.59 us
    pallas_call x1, Pallas kernels, body(): pl.pallas_call(moments_kernel, in_specs=[HBM] * 7, out_specs=[VMEM] * 4,...  4.3 us
    pallas_call x1, Pallas kernels, body(): pl.pallas_call(residual_kernel, in_specs=[VMEM] * 4, out_specs=[VMEM, VME...  1.92 us
  transfers between devices with their start and end apart: 1, of which 0 were waited for; matrix products, arithmetic and copies ran while one was open for 0% of the time, Pallas kernels for 1%

profile of v3, /device:TPU:1, one launch (start us, length us, event | category | flops | bytes accessed | tf_op | source)
XLA Modules:
  0.0 74.3 jit_solution(9151444883784566014)
XLA Ops:
  0.6 4.3 %moments.1 = (f32[32,72,128]{2,1,0:T(8,128)S(1)}, f32[80,128]{1,0:T(8,128)S(1)}, f32[4,40,4096]{2,1,0:T(8,128)S(1)}, f32[4,40,4096]{2,1,0:T(8,128)S(1)}) custom-call(s32[40]{0:T(128)} %ids_hbm.1, f32[2,5120]{1,0:T(2,128)} %pos_hbm.1, f32[4,40]{1,0:T(4,128)} %tput_hbm.1, s32[4,40]{1,0:T(4,128)} %sky_hbm.1, f32[4,40,4096]{2,1,0:T(8,128)} %flux_hbm.1, ...), custom_call_target="tpu_custom_call" | custom-call | flops 4000000000 | bytes 7864320 | tf_op jit(solution)/shard_map/moments/pallas_call | solution.py:327
  4.9 0.0 copy-start
  5.0 25.0 %all_to_all.15.in_ref = f32[16,144,128]{2,1,0:T(8,128)S(1)} all-to-all(f32[16,144,128]{2,1,0:T(8,128)S(1)} %bitcast.2), channel_id=1, replica_groups={{0,2,4,6,8,10,12,14,16,18,20,22,24,26,28,30},{32,34,36,38,40,42,44,46,4..., dimensions={0} | all-to-all | bytes 2359296 | tf_op jit(solution)/shard_map/all_to_all | solution.py:357
  29.9 0.1 add.1
  30.0 23.7 %all_to_all.16.in_ref = f32[8,144,128]{2,1,0:T(8,128)S(1)} all-to-all(f32[8,144,128]{2,1,0:T(8,128)S(1)} %add.1), channel_id=1, replica_groups={{0,32,64,96,128,160,192,224},{2,34,66,98,130,162,194,226},{4,36,68,100,..., dimensions={0} | all-to-all | bytes 1179648 | tf_op jit(solution)/shard_map/all_to_all | solution.py:364
  53.7 0.0 copy-done
  53.7 0.6 solve.1
  54.3 10.7 %all_to_all.17 = f32[16,32,128]{2,1,0:T(8,128)S(1)} all-to-all(f32[16,32,128]{2,1,0:T(8,128)S(1)} %solve.1), channel_id=1, replica_groups={{0,2,4,6,8,10,12,14,16,18,20,22,24,26,28,30},{32,34,36,38,40,42,44,46,4..., dimensions={0} | all-to-all | bytes 524288 | tf_op jit(solution)/shard_map/all_to_all | solution.py:371
  65.0 1.9 %residual.1 = (f32[8,160]{1,0:T(8,128)S(1)}, f32[4,40,2048]{2,1,0:T(8,128)S(1)}, f32[4,40,4096]{2,1,0:T(8,128)}, f32[16,4096]{1,0:T(8,128)}) custom-call(f32[80,128]{1,0:T(8,128)S(1)} %get-tuple-element.11.feat_ref, f32[32,16,128]{2,1,0:T(8,128)S(1)} %bitcast.3, f32[4,40,4096]{2,1,0:T(8,128)S(1)} %get-tuple-element.13.flux_ref, ...), custom_call_target="tpu_custom_call" | custom-call | flops 4000000000 | bytes 2621440 | tf_op jit(solution)/shard_map/residual/pallas_call | solution.py:374
  66.9 5.6 %collective-permute-start = (f32[8,160]{1,0:T(8,128)S(1)}, f32[8,160]{1,0:T(8,128)S(1)}, u32[]{:S(2)}, u32[]{:S(2)}) collective-permute-start(f32[8,160]{1,0:T(8,128)S(1)} %get-tuple-element.17.mine_ref), channel_id=1, source_target_pairs={{0,1},{1,0},{2,3},{3,2},{4,5},{5,4},{6,7},{7,6},{8,9},{9,8},{10,11... | collective-permute-start | bytes 15368 | tf_op jit(solution)/shard_map/ppermute | solution.py:396
  72.5 1.1 %late.1 = f32[4,40,4096]{2,1,0:T(8,128)} custom-call(f32[4,40,2048]{2,1,0:T(8,128)S(1)} %get-tuple-element.15.late_ref, f32[4,40,4096]{2,1,0:T(8,128)} %get-tuple-element.16._), custom_call_target="tpu_custom_call", output_to_operand_aliasing={{}: (1, {})} | custom-call | flops 4000000000 | bytes 2621440 | tf_op jit(solution)/shard_map/late/pallas_call | solution.py:397
  73.6 0.0 collective-permute-done.other_ref
  73.6 0.7 chi.1
Async XLA Ops:
  4.9 48.8 %copy-start = (f32[256,128]{1,0:T(8,128)S(1)}, f32[256,128]{1,0:T(8,128)}, u32[]{:S(2)}) copy-start(f32[256,128]{1,0:T(8,128)} %constant.2.clone.table_ref) | copy-start | bytes 393220
  66.9 6.7 %collective-permute-start = (f32[8,160]{1,0:T(8,128)S(1)}, f32[8,160]{1,0:T(8,128)S(1)}, u32[]{:S(2)}, u32[]{:S(2)}) collective-permute-start(f32[8,160]{1,0:T(8,128)S(1)} %get-tuple-element.17.mine_ref), channel_id=1, source_target_pairs={{0,1},{1,0},{2,3},{3,2},{4,5},{5,4},{6,7},{7,6},{8,9},{9,8},{10,11... | collective-permute-start | bytes 15368 | tf_op jit(solution)/shard_map/ppermute | solution.py:396

commit v4 on v3

--- a/solution.py
+++ b/solution.py
@@ -12,10 +12,10 @@
 PRIOR = 1.0
 MOMENTS = 7
 BASIS = 4
-RIGHT_ROW = 56
-PACKED = 72
+RIGHT_ROW = 49
+PACKED = 65
+ROWS = 72
 LANES = 128
-PAIR = 1
 PIECE = 512
 WRITE = 1024
 EARLY = 2048
@@ -169,7 +169,8 @@
         right = jnp.concatenate([high, high, high, middle, middle, low], axis=0)
         sums = jnp.dot(left_ref[:, 0:right.shape[0]], right, preferred_element_type=jnp.float32)
         for k in range(PIECE // LANES):
-            out_ref[piece * (PIECE // LANES) + k] = sums[0:PACKED, k * LANES:(k + 1) * LANES]
+            chunk = piece * (PIECE // LANES) + k
+            out_ref[chunk * PACKED:(chunk + 1) * PACKED, :] = sums[0:PACKED, k * LANES:(k + 1) * LANES]
 
 
 def moments_kernel(ids_hbm, pos_hbm, tput_hbm, sky_hbm, flux_hbm, ivar_hbm, bits_hbm, out_ref, feat_ref, flux_ref, weight_ref,
@@ -191,16 +192,19 @@
 
 
 def add_kernel(in_ref, out_ref):
+    total = in_ref[0:PACKED, :]
+    for source in range(1, in_ref.shape[0] // PACKED):
+        total = total + in_ref[source * PACKED:(source + 1) * PACKED, :]
+    total = jnp.concatenate([total, jnp.zeros((ROWS - PACKED, LANES), jnp.float32)], axis=0)
+    for target in range(out_ref.shape[0]):
+        out_ref[target] = total
+
+
+def solve_kernel(in_ref, table_ref, out_ref):
     total = in_ref[0]
     for source in range(1, in_ref.shape[0]):
         total = total + in_ref[source]
-    for target in range(out_ref.shape[0]):
-        out_ref[target] = total
-
-
-def solve_one(total, table):
-    moments = jnp.concatenate([total[0:RIGHT_ROW], jnp.zeros((LANES - RIGHT_ROW, LANES), jnp.float32)], axis=0)
-    normal = dot6(table, moments)
+    normal = dot6(table_ref[...], jnp.concatenate([total, jnp.zeros((LANES - ROWS, LANES), jnp.float32)], axis=0))
     sub = lax.broadcasted_iota(jnp.int32, (PARAMS, LANES), 0)
     columns = []
     for k in range(PARAMS):
@@ -215,16 +219,7 @@
         for l in range(j + 1, PARAMS):
             columns[l] = columns[l] - factor * columns[l][j:j + 1]
         right = right - factor * right[j:j + 1]
-    return right * scale
-
-
-def solve_kernel(in_ref, table_ref, out_ref):
-    total = in_ref[0]
-    for source in range(1, in_ref.shape[0]):
-        total = total + in_ref[source]
-    table = table_ref[...]
-    stretches = in_ref.shape[1] // PACKED
-    solved = jnp.concatenate([solve_one(total[t * PACKED:(t + 1) * PACKED], table) for t in range(stretches)], axis=0)
+    solved = right * scale
     for target in range(out_ref.shape[0]):
         out_ref[target] = solved
 
@@ -303,7 +298,7 @@
     def place(z, y, x):
         return (z * ny + y) * nx + x
 
-    pair = PAIR
+    pair = 2
     near = [[place(q * pair + h, y, x) for h in range(pair) for y in range(ny) for x in range(nx)] for q in range(nz // pair)]
     far = [[place(q * pair + h, y, x) for q in range(nz // pair)] for h in range(pair) for y in range(ny) for x in range(nx)]
     return near, far
@@ -329,7 +324,7 @@
             in_specs=[HBM] * 7,
             out_specs=[VMEM] * 4,
             out_shape=[
-                jax.ShapeDtypeStruct((waves // LANES, PACKED, LANES), f32),
+                jax.ShapeDtypeStruct((waves // LANES * PACKED, LANES), f32),
                 jax.ShapeDtypeStruct((2 * fibers, LANES), f32),
                 jax.ShapeDtypeStruct(spectra.shape, f32),
                 jax.ShapeDtypeStruct(spectra.shape, f32),
@@ -352,24 +347,22 @@
         )(*held)
 
         members = len(near[0])
-        rows = waves // LANES // members * PACKED
-        packed = packed.reshape(members, rows, LANES)
+        packed = packed.reshape(members, PACKED, 1, LANES)
         arrived = lax.all_to_all(packed, "fiber", 0, 0, axis_index_groups=near, tiled=True)
         copies = pl.pallas_call(
             add_kernel,
-            out_shape=jax.ShapeDtypeStruct((len(far[0]), rows, LANES), f32),
+            out_shape=jax.ShapeDtypeStruct((len(far[0]), ROWS, LANES), f32),
             compiler_params=params(8),
             name="add",
-        )(arrived)
+        )(arrived.reshape(members * PACKED, LANES))
         parts = lax.all_to_all(copies, "fiber", 0, 0, axis_index_groups=far, tiled=True)
         solved = pl.pallas_call(
             solve_kernel,
-            out_shape=jax.ShapeDtypeStruct((members, rows // PACKED * PARAMS, LANES), f32),
+            out_shape=jax.ShapeDtypeStruct((members, PARAMS, LANES), f32),
             compiler_params=params(8),
             name="solve",
         )(parts, jnp.asarray(rebuild_rows(), f32))
         coeffs = lax.all_to_all(solved, "fiber", 0, 0, axis_index_groups=near, tiled=True)
-        coeffs = coeffs.reshape(waves // LANES, PARAMS, LANES)
 
         chi_local, late, residual, sky_coeffs = pl.pallas_call(
             residual_kernel,

time: 74.5 us -> 66.9 us (0.90)
  blocking collectives: 59.4 us -> 53 us
  starting transfers between devices: 5.59 us -> 4.5 us
    all_to_all x1, blocking collectives: 23.7 us -> 15.1 us  [body(): lax.all_to_all(copies, 'fiber', 0, 0, axis_index_groups=far, tiled=True)]
    all_to_all x1, blocking collectives: 25 us -> 26.1 us  [body(): lax.all_to_all(packed, 'fiber', 0, 0, axis_index_groups=near, tiled=True)]
    ppermute x1, starting transfers between devices: 5.59 us -> 4.5 us  [body(): lax.ppermute(chi_local, 'wave', [(h, (h + 1) % halves) for h in range(hal...]
    all_to_all x1, blocking collectives: 10.7 us -> 11.7 us  [body(): lax.all_to_all(solved, 'fiber', 0, 0, axis_index_groups=near, tiled=True)]
  transfers between devices with their start and end apart: 1 -> 1, of which waited for: 0 -> 0; matrix products, arithmetic and copies ran while one was open for 0% -> 0% of each run, Pallas kernels for 1% -> 2%
where the time goes in v4:
time: 66.9 us; the launch traced here: 66.7 us
  blocking collectives  53 us (79%)
  Pallas kernels  8.48 us (13%)
  starting transfers between devices  4.5 us (7%)
  between operations  0.68 us (1%)
    all_to_all x1, blocking collectives, body(): lax.all_to_all(packed, 'fiber', 0, 0, axis_index_groups=near, tiled=True)  26.1 us
    all_to_all x1, blocking collectives, body(): lax.all_to_all(copies, 'fiber', 0, 0, axis_index_groups=far, tiled=True)  15.1 us
    all_to_all x1, blocking collectives, body(): lax.all_to_all(solved, 'fiber', 0, 0, axis_index_groups=near, tiled=True)  11.7 us
    ppermute x1, starting transfers between devices, body(): lax.ppermute(chi_local, 'wave', [(h, (h + 1) % halves) for h in range(hal...  4.5 us
    pallas_call x1, Pallas kernels, body(): pl.pallas_call(moments_kernel, in_specs=[HBM] * 7, out_specs=[VMEM] * 4,...  4.31 us
    pallas_call x1, Pallas kernels, body(): pl.pallas_call(residual_kernel, in_specs=[VMEM] * 4, out_specs=[VMEM, VME...  1.92 us
  transfers between devices with their start and end apart: 1, of which 0 were waited for; matrix products, arithmetic and copies ran while one was open for 0% of the time, Pallas kernels for 2%

profile of v4, /device:TPU:1, one launch (start us, length us, event | category | flops | bytes accessed | tf_op | source)
XLA Modules:
  0.0 66.7 jit_solution(12357889022188263417)
XLA Ops:
  0.6 4.3 %moments.1 = (f32[2080,128]{1,0:T(8,128)S(1)}, f32[80,128]{1,0:T(8,128)S(1)}, f32[4,40,4096]{2,1,0:T(8,128)S(1)}, f32[4,40,4096]{2,1,0:T(8,128)S(1)}) custom-call(s32[40]{0:T(128)} %ids_hbm.1, f32[2,5120]{1,0:T(2,128)} %pos_hbm.1, f32[4,40]{1,0:T(4,128)} %tput_hbm.1, s32[4,40]{1,0:T(4,128)} %sky_hbm.1, f32[4,40,4096]{2,1,0:T(8,128)} %flux_hbm.1, ...), custom_call_target="tpu_custom_call" | custom-call | flops 4000000000 | bytes 7864320 | tf_op jit(solution)/shard_map/moments/pallas_call | solution.py:322
  4.9 0.0 copy-start
  5.0 26.1 %all_to_all.15 = f32[32,65,1,128]{3,2,1,0:T(1,128)S(1)} all-to-all(f32[32,65,1,128]{3,2,1,0:T(1,128)S(1)} %bitcast.3), channel_id=1, replica_groups={{0,2,4,6,8,10,12,14,16,18,20,22,24,26,28,30,32,34,36,38,40,42,44,46,48,..., dimensions={0} | all-to-all | bytes 2129920 | tf_op jit(solution)/shard_map/all_to_all | solution.py:351
  31.1 0.1 add.1
  31.2 15.1 %all_to_all.16.in_ref = f32[4,72,128]{2,1,0:T(8,128)S(1)} all-to-all(f32[4,72,128]{2,1,0:T(8,128)S(1)} %add.1), channel_id=1, replica_groups={{0,64,128,192},{2,66,130,194},{4,68,132,196},{6,70,134,198},{8,72,136,2..., dimensions={0} | all-to-all | bytes 294912 | tf_op jit(solution)/shard_map/all_to_all | solution.py:358
  46.3 0.0 copy-done
  46.3 0.4 solve.1
  46.8 11.7 %all_to_all.17.coeff_ref = f32[32,16,128]{2,1,0:T(8,128)S(1)} all-to-all(f32[32,16,128]{2,1,0:T(8,128)S(1)} %solve.1), channel_id=1, replica_groups={{0,2,4,6,8,10,12,14,16,18,20,22,24,26,28,30,32,34,36,38,40,42,44,46,48,..., dimensions={0} | all-to-all | bytes 524288 | tf_op jit(solution)/shard_map/all_to_all | solution.py:365
  58.5 1.9 %residual.1 = (f32[8,160]{1,0:T(8,128)S(1)}, f32[4,40,2048]{2,1,0:T(8,128)S(1)}, f32[4,40,4096]{2,1,0:T(8,128)}, f32[16,4096]{1,0:T(8,128)}) custom-call(f32[80,128]{1,0:T(8,128)S(1)} %get-tuple-element.11.feat_ref, f32[32,16,128]{2,1,0:T(8,128)S(1)} %all_to_all.17.coeff_ref, f32[4,40,4096]{2,1,0:T(8,128)S(1)} %get-tuple-element.13.flux_ref, ...), custom_call_target="tpu_custom_call" | custom-call | flops 4000000000 | bytes 2621440 | tf_op jit(solution)/shard_map/residual/pallas_call | solution.py:367
  60.4 4.5 %collective-permute-start = (f32[8,160]{1,0:T(8,128)S(1)}, f32[8,160]{1,0:T(8,128)S(1)}, u32[]{:S(2)}, u32[]{:S(2)}) collective-permute-start(f32[8,160]{1,0:T(8,128)S(1)} %get-tuple-element.17.mine_ref), channel_id=1, source_target_pairs={{0,1},{1,0},{2,3},{3,2},{4,5},{5,4},{6,7},{7,6},{8,9},{9,8},{10,11... | collective-permute-start | bytes 15368 | tf_op jit(solution)/shard_map/ppermute | solution.py:389
  64.9 1.1 %late.1 = f32[4,40,4096]{2,1,0:T(8,128)} custom-call(f32[4,40,2048]{2,1,0:T(8,128)S(1)} %get-tuple-element.15.late_ref, f32[4,40,4096]{2,1,0:T(8,128)} %get-tuple-element.16._), custom_call_target="tpu_custom_call", output_to_operand_aliasing={{}: (1, {})} | custom-call | flops 4000000000 | bytes 2621440 | tf_op jit(solution)/shard_map/late/pallas_call | solution.py:390
  66.0 0.0 collective-permute-done.other_ref
  66.0 0.7 chi.1
Async XLA Ops:
  4.9 41.4 %copy-start = (f32[256,128]{1,0:T(8,128)S(1)}, f32[256,128]{1,0:T(8,128)}, u32[]{:S(2)}) copy-start(f32[256,128]{1,0:T(8,128)} %constant.2.clone.table_ref) | copy-start | bytes 393220
  60.4 5.6 %collective-permute-start = (f32[8,160]{1,0:T(8,128)S(1)}, f32[8,160]{1,0:T(8,128)S(1)}, u32[]{:S(2)}, u32[]{:S(2)}) collective-permute-start(f32[8,160]{1,0:T(8,128)S(1)} %get-tuple-element.17.mine_ref), channel_id=1, source_target_pairs={{0,1},{1,0},{2,3},{3,2},{4,5},{5,4},{6,7},{7,6},{8,9},{9,8},{10,11... | collective-permute-start | bytes 15368 | tf_op jit(solution)/shard_map/ppermute | solution.py:389

commit v5 on v4

--- a/solution.py
+++ b/solution.py
@@ -18,8 +18,8 @@
 LANES = 128
 PIECE = 512
 WRITE = 1024
-EARLY = 2048
-GRAIN = 2048
+EARLY = 3072
+GRAINS = (2048, 1024, 1024)
 FLOPS = 4_000_000_000
 
 
@@ -111,17 +111,25 @@
     series_x = legendre_series(jnp.broadcast_to(coord_x, (fibers, LANES)), MOMENTS)
     series_y = legendre_series(jnp.broadcast_to(coord_y, (fibers, LANES)), MOMENTS)
     is_right = lane >= RIGHT_ROW
-    index_x = jnp.where(is_right, (lane - RIGHT_ROW) // BASIS, lane // MOMENTS)
-    index_y = jnp.where(is_right, (lane - RIGHT_ROW) % BASIS, lane % MOMENTS)
-    along_x = jnp.zeros((fibers, LANES), jnp.float32)
-    along_y = jnp.zeros((fibers, LANES), jnp.float32)
-    for order in range(MOMENTS):
-        along_x = jnp.where(index_x == order, series_x[order], along_x)
-        along_y = jnp.where(index_y == order, series_y[order], along_y)
-    product = along_x * along_y
+
+    def products(index_x, index_y):
+        along_x = jnp.zeros((fibers, LANES), jnp.float32)
+        along_y = jnp.zeros((fibers, LANES), jnp.float32)
+        for order in range(MOMENTS):
+            along_x = jnp.where(index_x == order, series_x[order], along_x)
+            along_y = jnp.where(index_y == order, series_y[order], along_y)
+        return along_x * along_y
+
+    product = products(
+        jnp.where(is_right, (lane - RIGHT_ROW) // BASIS, lane // MOMENTS),
+        jnp.where(is_right, (lane - RIGHT_ROW) % BASIS, lane % MOMENTS),
+    )
+    group = lane // PARAMS
+    model_parts = [part.astype(jnp.float32) for part in split3(products(lane % PARAMS // BASIS, lane % BASIS))]
+    model_left = jnp.where((group == 1) | (group == 4), model_parts[1], jnp.where(group == 2, model_parts[2], model_parts[0]))
     moment_part = jnp.where(lane < MOMENTS * MOMENTS, product, 0.0)
     right_part = jnp.where(is_right & (lane < RIGHT_ROW + PARAMS), product, 0.0)
-    feat_ref[0:fibers, :] = right_part
+    feat_ref[0:fibers, :] = model_left
     feat_ref[fibers:2 * fibers, :] = turned[0:fibers, :]
     both = jnp.concatenate([moment_part, right_part], axis=0)
     high, middle, low = (part.astype(jnp.float32) for part in split3(both))
@@ -135,13 +143,15 @@
 
 
 def piece_copies(flux_hbm, ivar_hbm, bits_hbm, flux_ref, ivar_ref, bits_ref, sems):
-    copies = []
-    for piece in range(flux_ref.shape[2] // GRAIN):
-        cut = pl.ds(piece * GRAIN, GRAIN)
-        copies.append([
-            pltpu.make_async_copy(source.at[:, :, cut], target.at[:, :, cut], sems.at[piece, which])
+    copies = {}
+    begin = 0
+    for place, width in enumerate(GRAINS):
+        cut = pl.ds(begin, width)
+        copies[begin] = [
+            pltpu.make_async_copy(source.at[:, :, cut], target.at[:, :, cut], sems.at[place, which])
             for which, (source, target) in enumerate(((flux_hbm, flux_ref), (ivar_hbm, ivar_ref), (bits_hbm, bits_ref)))
-        ])
+        ]
+        begin += width
     return copies
 
 
@@ -149,9 +159,8 @@
     exposures, fibers, _ = flux_ref.shape
     columns = feat_ref[fibers:2 * fibers, :]
     for piece in range(flux_ref.shape[2] // PIECE):
-        if piece * PIECE % GRAIN == 0:
-            for copy in copies[piece * PIECE // GRAIN]:
-                copy.wait()
+        for copy in copies.get(piece * PIECE, ()):
+            copy.wait()
         here = slice(piece * PIECE, (piece + 1) * PIECE)
         moment_rows = None
         right_rows = None
@@ -182,9 +191,9 @@
     for copy in small:
         copy.start()
     copies = piece_copies(flux_hbm, ivar_hbm, bits_hbm, flux_ref, ivar_ref, bits_ref, sems)
-    for place, trio in enumerate(copies):
+    for begin, trio in copies.items():
         for which, copy in enumerate(trio):
-            copy.start(priority=(place + which) % 2)
+            copy.start(priority=(which + (begin > 0)) % 2)
     for copy in small:
         copy.wait()
     build_features(ids_ref, pos_ref, tput_ref, sky_ref, stack_ref, feat_ref, left_ref)
@@ -235,11 +244,12 @@
     all_ref[...] = joined(coeff_ref, 0, chunks)
     copies = [pltpu.make_async_copy(all_ref, all_hbm, all_sem)]
     copies[0].start(priority=1)
-    basis = feat_ref[0:fibers, RIGHT_ROW:RIGHT_ROW + PARAMS]
+    basis = feat_ref[0:fibers, 0:6 * PARAMS].astype(jnp.bfloat16)
     sums = [None] * exposures
     for piece in range(waves // PIECE):
         here = slice(piece * PIECE, (piece + 1) * PIECE)
-        model = dot6(basis, joined(coeff_ref, piece * (PIECE // LANES), PIECE // LANES))
+        high, middle, low = split3(joined(coeff_ref, piece * (PIECE // LANES), PIECE // LANES))
+        model = jnp.dot(basis, jnp.concatenate([high, high, high, middle, middle, low], axis=0), preferred_element_type=jnp.float32)
         for e in range(exposures):
             residual = flux_ref[e, :, here] - feat_ref[fibers:2 * fibers, e:e + 1] * model
             if piece * PIECE < early:
@@ -339,7 +349,7 @@
                 pltpu.VMEM((80, stacked), jnp.bfloat16),
                 pltpu.VMEM((stacked, LANES), f32),
                 pltpu.SemaphoreType.DMA((4,)),
-                pltpu.SemaphoreType.DMA((waves // GRAIN, 3)),
+                pltpu.SemaphoreType.DMA((len(GRAINS), 3)),
             ],
             compiler_params=params(20),
             cost_estimate=cost(FLOPS, 3 * moved),

time: 66.9 us -> 66.9 us (level)
  transfers between devices with their start and end apart: 1 -> 1, of which waited for: 0 -> 0; matrix products, arithmetic and copies ran while one was open for 0% -> 0% of each run, Pallas kernels for 2% -> 1%
where the time goes in v5:
time: 66.9 us; the launch traced here: 66.7 us
  blocking collectives  53 us (79%)
  Pallas kernels  8.45 us (13%)
  starting transfers between devices  4.51 us (7%)
  between operations  0.68 us (1%)
    all_to_all x1, blocking collectives, body(): lax.all_to_all(packed, 'fiber', 0, 0, axis_index_groups=near, tiled=True)  26.1 us
    all_to_all x1, blocking collectives, body(): lax.all_to_all(copies, 'fiber', 0, 0, axis_index_groups=far, tiled=True)  15.1 us
    all_to_all x1, blocking collectives, body(): lax.all_to_all(solved, 'fiber', 0, 0, axis_index_groups=near, tiled=True)  11.7 us
    ppermute x1, starting transfers between devices, body(): lax.ppermute(chi_local, 'wave', [(h, (h + 1) % halves) for h in range(hal...  4.51 us
    pallas_call x1, Pallas kernels, body(): pl.pallas_call(moments_kernel, in_specs=[HBM] * 7, out_specs=[VMEM] * 4,...  4.48 us
    pallas_call x1, Pallas kernels, body(): pl.pallas_call(residual_kernel, in_specs=[VMEM] * 4, out_specs=[VMEM, VME...  1.94 us
  transfers between devices with their start and end apart: 1, of which 0 were waited for; matrix products, arithmetic and copies ran while one was open for 0% of the time, Pallas kernels for 1%

profile of v5, /device:TPU:1, one launch (start us, length us, event | category | flops | bytes accessed | tf_op | source)
XLA Modules:
  0.0 66.7 jit_solution(4266235222459413460)
XLA Ops:
  0.6 4.5 %moments.1 = (f32[2080,128]{1,0:T(8,128)S(1)}, f32[80,128]{1,0:T(8,128)S(1)}, f32[4,40,4096]{2,1,0:T(8,128)S(1)}, f32[4,40,4096]{2,1,0:T(8,128)S(1)}) custom-call(s32[40]{0:T(128)} %ids_hbm.1, f32[2,5120]{1,0:T(2,128)} %pos_hbm.1, f32[4,40]{1,0:T(4,128)} %tput_hbm.1, s32[4,40]{1,0:T(4,128)} %sky_hbm.1, f32[4,40,4096]{2,1,0:T(8,128)} %flux_hbm.1, ...), custom_call_target="tpu_custom_call" | custom-call | flops 4000000000 | bytes 7864320 | tf_op jit(solution)/shard_map/moments/pallas_call | solution.py:332
  5.1 0.0 copy-start
  5.1 26.1 %all_to_all.15 = f32[32,65,1,128]{3,2,1,0:T(1,128)S(1)} all-to-all(f32[32,65,1,128]{3,2,1,0:T(1,128)S(1)} %bitcast.3), channel_id=1, replica_groups={{0,2,4,6,8,10,12,14,16,18,20,22,24,26,28,30,32,34,36,38,40,42,44,46,48,..., dimensions={0} | all-to-all | bytes 2129920 | tf_op jit(solution)/shard_map/all_to_all | solution.py:361
  31.3 0.1 add.1
  31.3 15.1 %all_to_all.16.in_ref = f32[4,72,128]{2,1,0:T(8,128)S(1)} all-to-all(f32[4,72,128]{2,1,0:T(8,128)S(1)} %add.1), channel_id=1, replica_groups={{0,64,128,192},{2,66,130,194},{4,68,132,196},{6,70,134,198},{8,72,136,2..., dimensions={0} | all-to-all | bytes 294912 | tf_op jit(solution)/shard_map/all_to_all | solution.py:368
  46.5 0.0 copy-done
  46.5 0.4 solve.1
  46.9 11.7 %all_to_all.17.coeff_ref = f32[32,16,128]{2,1,0:T(8,128)S(1)} all-to-all(f32[32,16,128]{2,1,0:T(8,128)S(1)} %solve.1), channel_id=1, replica_groups={{0,2,4,6,8,10,12,14,16,18,20,22,24,26,28,30,32,34,36,38,40,42,44,46,48,..., dimensions={0} | all-to-all | bytes 524288 | tf_op jit(solution)/shard_map/all_to_all | solution.py:375
  58.7 1.9 %residual.1 = (f32[8,160]{1,0:T(8,128)S(1)}, f32[4,40,1024]{2,1,0:T(8,128)S(1)}, f32[4,40,4096]{2,1,0:T(8,128)}, f32[16,4096]{1,0:T(8,128)}) custom-call(f32[80,128]{1,0:T(8,128)S(1)} %get-tuple-element.11.feat_ref, f32[32,16,128]{2,1,0:T(8,128)S(1)} %all_to_all.17.coeff_ref, f32[4,40,4096]{2,1,0:T(8,128)S(1)} %get-tuple-element.13.flux_ref, ...), custom_call_target="tpu_custom_call" | custom-call | flops 4000000000 | bytes 2621440 | tf_op jit(solution)/shard_map/residual/pallas_call | solution.py:377
  60.6 4.5 %collective-permute-start = (f32[8,160]{1,0:T(8,128)S(1)}, f32[8,160]{1,0:T(8,128)S(1)}, u32[]{:S(2)}, u32[]{:S(2)}) collective-permute-start(f32[8,160]{1,0:T(8,128)S(1)} %get-tuple-element.17.mine_ref), channel_id=1, source_target_pairs={{0,1},{1,0},{2,3},{3,2},{4,5},{5,4},{6,7},{7,6},{8,9},{9,8},{10,11... | collective-permute-start | bytes 15368 | tf_op jit(solution)/shard_map/ppermute | solution.py:399
  65.1 0.9 %late.1 = f32[4,40,4096]{2,1,0:T(8,128)} custom-call(f32[4,40,1024]{2,1,0:T(8,128)S(1)} %get-tuple-element.15.late_ref, f32[4,40,4096]{2,1,0:T(8,128)} %get-tuple-element.16._), custom_call_target="tpu_custom_call", output_to_operand_aliasing={{}: (1, {})} | custom-call | flops 4000000000 | bytes 2621440 | tf_op jit(solution)/shard_map/late/pallas_call | solution.py:400
  66.0 0.0 collective-permute-done.other_ref
  66.0 0.7 chi.1
Async XLA Ops:
  5.1 41.4 %copy-start = (f32[256,128]{1,0:T(8,128)S(1)}, f32[256,128]{1,0:T(8,128)}, u32[]{:S(2)}) copy-start(f32[256,128]{1,0:T(8,128)} %constant.2.clone.table_ref) | copy-start | bytes 393220
  60.6 5.4 %collective-permute-start = (f32[8,160]{1,0:T(8,128)S(1)}, f32[8,160]{1,0:T(8,128)S(1)}, u32[]{:S(2)}, u32[]{:S(2)}) collective-permute-start(f32[8,160]{1,0:T(8,128)S(1)} %get-tuple-element.17.mine_ref), channel_id=1, source_target_pairs={{0,1},{1,0},{2,3},{3,2},{4,5},{5,4},{6,7},{7,6},{8,9},{9,8},{10,11... | collective-permute-start | bytes 15368 | tf_op jit(solution)/shard_map/ppermute | solution.py:399

commit v6 on v5

--- a/solution.py
+++ b/solution.py
@@ -18,8 +18,9 @@
 LANES = 128
 PIECE = 512
 WRITE = 1024
-EARLY = 3072
-GRAINS = (2048, 1024, 1024)
+EARLY = 1024
+MIDDLE = 1536
+GRAINS = (2048, 2048)
 FLOPS = 4_000_000_000
 
 
@@ -273,24 +274,34 @@
         copy.wait()
 
 
-def late_kernel(late_ref, _, res_hbm, sems):
-    width = late_ref.shape[2]
-    begin = res_hbm.shape[2] - width
-    copies = [
-        pltpu.make_async_copy(late_ref.at[e], res_hbm.at[e, :, pl.ds(begin, width)], sems.at[e])
+def late_copies(late_ref, res_hbm, first, width, sems):
+    begin = res_hbm.shape[2] - late_ref.shape[2] + first
+    return [
+        pltpu.make_async_copy(late_ref.at[e, :, pl.ds(first, width)], res_hbm.at[e, :, pl.ds(begin, width)], sems.at[e])
         for e in range(late_ref.shape[0])
     ]
+
+
+def middle_kernel(late_ref, _, res_hbm, sems):
+    copies = late_copies(late_ref, res_hbm, 0, MIDDLE, sems)
     for e, copy in enumerate(copies):
         copy.start(priority=e % 2)
     for copy in copies:
         copy.wait()
 
 
-def chi_kernel(scale, mine_ref, other_ref, out_ref):
+def finish_kernel(scale, late_ref, mine_ref, other_ref, _, res_hbm, out_hbm, out_ref, sems, out_sem):
+    copies = late_copies(late_ref, res_hbm, MIDDLE, late_ref.shape[2] - MIDDLE, sems)
+    for e, copy in enumerate(copies):
+        copy.start(priority=e % 2)
     exposures, fibers = out_ref.shape
     total = (mine_ref[...] + other_ref[...]) * scale
     for e in range(exposures):
         out_ref[e:e + 1, :] = total[0:1, e * fibers:(e + 1) * fibers]
+    copies.append(pltpu.make_async_copy(out_ref, out_hbm, out_sem))
+    copies[-1].start(priority=1)
+    for copy in copies:
+        copy.wait()
 
 
 def cost(flops, moved):
@@ -398,7 +409,7 @@
         halves = lax.axis_size("wave")
         chi_other = lax.ppermute(chi_local, "wave", [(h, (h + 1) % halves) for h in range(halves)])
         residual = pl.pallas_call(
-            late_kernel,
+            middle_kernel,
             in_specs=[VMEM, HBM],
             out_specs=HBM,
             out_shape=jax.ShapeDtypeStruct(spectra.shape, f32),
@@ -406,14 +417,25 @@
             scratch_shapes=[pltpu.SemaphoreType.DMA((exposures,))],
             compiler_params=params(4),
             cost_estimate=cost(FLOPS, moved),
-            name="late",
+            name="middle",
         )(late, residual)
-        chi_square = pl.pallas_call(
-            functools.partial(chi_kernel, 1.0 / (waves * halves)),
-            out_shape=jax.ShapeDtypeStruct((exposures, fibers), f32),
+        residual, chi_square = pl.pallas_call(
+            functools.partial(finish_kernel, 1.0 / (waves * halves)),
+            in_specs=[VMEM, VMEM, VMEM, HBM],
+            out_specs=[HBM, HBM],
+            out_shape=[
+                jax.ShapeDtypeStruct(spectra.shape, f32),
+                jax.ShapeDtypeStruct((exposures, fibers), f32),
+            ],
+            input_output_aliases={3: 0},
+            scratch_shapes=[
+                pltpu.VMEM((exposures, fibers), f32),
+                pltpu.SemaphoreType.DMA((exposures,)),
+                pltpu.SemaphoreType.DMA,
+            ],
             compiler_params=params(4),
-            name="chi",
-        )(chi_local, chi_other)
+            name="finish",
+        )(late, chi_local, chi_other, residual)
         return residual, chi_square, sky_coeffs
 
     return body

time: 66.9 us -> 66.8 us (level)
  no operation moved by 1% of the time
where the time goes in v6:
time: 66.8 us; the launch traced here: 66.6 us
  blocking collectives  53 us (79%)
  Pallas kernels  8.43 us (13%)
  starting transfers between devices  4.51 us (7%)
  between operations  0.68 us (1%)
    all_to_all x1, blocking collectives, body(): lax.all_to_all(packed, 'fiber', 0, 0, axis_index_groups=near, tiled=True)  26.1 us
    all_to_all x1, blocking collectives, body(): lax.all_to_all(copies, 'fiber', 0, 0, axis_index_groups=far, tiled=True)  15.1 us
    all_to_all x1, blocking collectives, body(): lax.all_to_all(solved, 'fiber', 0, 0, axis_index_groups=near, tiled=True)  11.7 us
    ppermute x1, starting transfers between devices, body(): lax.ppermute(chi_local, 'wave', [(h, (h + 1) % halves) for h in range(hal...  4.51 us
    pallas_call x1, Pallas kernels, body(): pl.pallas_call(moments_kernel, in_specs=[HBM] * 7, out_specs=[VMEM] * 4,...  4.31 us
    pallas_call x1, Pallas kernels, body(): pl.pallas_call(residual_kernel, in_specs=[VMEM] * 4, out_specs=[VMEM, VME...  1.64 us
  transfers between devices with their start and end apart: 1, of which 0 were waited for; matrix products, arithmetic and copies ran while one was open for 0% of the time, Pallas kernels for 1%

profile of v6, /device:TPU:1, one launch (start us, length us, event | category | flops | bytes accessed | tf_op | source)
XLA Modules:
  0.0 66.6 jit_solution(9276494236444565831)
XLA Ops:
  0.6 4.3 %moments.1 = (f32[2080,128]{1,0:T(8,128)S(1)}, f32[80,128]{1,0:T(8,128)S(1)}, f32[4,40,4096]{2,1,0:T(8,128)S(1)}, f32[4,40,4096]{2,1,0:T(8,128)S(1)}) custom-call(s32[40]{0:T(128)} %ids_hbm.1, f32[2,5120]{1,0:T(2,128)} %pos_hbm.1, f32[4,40]{1,0:T(4,128)} %tput_hbm.1, s32[4,40]{1,0:T(4,128)} %sky_hbm.1, f32[4,40,4096]{2,1,0:T(8,128)} %flux_hbm.1, ...), custom_call_target="tpu_custom_call" | custom-call | flops 4000000000 | bytes 7864320 | tf_op jit(solution)/shard_map/moments/pallas_call | solution.py:343
  4.9 0.0 copy-start
  5.0 26.1 %all_to_all.15 = f32[32,65,1,128]{3,2,1,0:T(1,128)S(1)} all-to-all(f32[32,65,1,128]{3,2,1,0:T(1,128)S(1)} %bitcast.3), channel_id=1, replica_groups={{0,2,4,6,8,10,12,14,16,18,20,22,24,26,28,30,32,34,36,38,40,42,44,46,48,..., dimensions={0} | all-to-all | bytes 2129920 | tf_op jit(solution)/shard_map/all_to_all | solution.py:372
  31.1 0.1 add.1
  31.2 15.1 %all_to_all.16.in_ref = f32[4,72,128]{2,1,0:T(8,128)S(1)} all-to-all(f32[4,72,128]{2,1,0:T(8,128)S(1)} %add.1), channel_id=1, replica_groups={{0,64,128,192},{2,66,130,194},{4,68,132,196},{6,70,134,198},{8,72,136,2..., dimensions={0} | all-to-all | bytes 294912 | tf_op jit(solution)/shard_map/all_to_all | solution.py:379
  46.3 0.0 copy-done
  46.3 0.4 solve.1
  46.8 11.7 %all_to_all.17.coeff_ref = f32[32,16,128]{2,1,0:T(8,128)S(1)} all-to-all(f32[32,16,128]{2,1,0:T(8,128)S(1)} %solve.1), channel_id=1, replica_groups={{0,2,4,6,8,10,12,14,16,18,20,22,24,26,28,30,32,34,36,38,40,42,44,46,48,..., dimensions={0} | all-to-all | bytes 524288 | tf_op jit(solution)/shard_map/all_to_all | solution.py:386
  58.5 1.6 %residual.1 = (f32[8,160]{1,0:T(8,128)S(1)}, f32[4,40,3072]{2,1,0:T(8,128)S(1)}, f32[4,40,4096]{2,1,0:T(8,128)}, f32[16,4096]{1,0:T(8,128)}) custom-call(f32[80,128]{1,0:T(8,128)S(1)} %get-tuple-element.13.feat_ref, f32[32,16,128]{2,1,0:T(8,128)S(1)} %all_to_all.17.coeff_ref, f32[4,40,4096]{2,1,0:T(8,128)S(1)} %get-tuple-element.15.flux_ref, ...), custom_call_target="tpu_custom_call" | custom-call | flops 4000000000 | bytes 2621440 | tf_op jit(solution)/shard_map/residual/pallas_call | solution.py:388
  60.2 4.5 %collective-permute-start = (f32[8,160]{1,0:T(8,128)S(1)}, f32[8,160]{1,0:T(8,128)S(1)}, u32[]{:S(2)}, u32[]{:S(2)}) collective-permute-start(f32[8,160]{1,0:T(8,128)S(1)} %get-tuple-element.18.mine_ref), channel_id=1, source_target_pairs={{0,1},{1,0},{2,3},{3,2},{4,5},{5,4},{6,7},{7,6},{8,9},{9,8},{10,11... | collective-permute-start | bytes 15368 | tf_op jit(solution)/shard_map/ppermute | solution.py:410
  64.7 1.0 %middle.1._ = f32[4,40,4096]{2,1,0:T(8,128)} custom-call(f32[4,40,3072]{2,1,0:T(8,128)S(1)} %get-tuple-element.17.late_ref, f32[4,40,4096]{2,1,0:T(8,128)} %get-tuple-element.19._), custom_call_target="tpu_custom_call", output_to_operand_aliasing={{}: (1, {})} | custom-call | flops 4000000000 | bytes 2621440 | tf_op jit(solution)/shard_map/middle/pallas_call | solution.py:411
  65.6 0.0 collective-permute-done.other_ref
  65.7 1.0 %finish.1 = (f32[4,40,4096]{2,1,0:T(8,128)}, f32[4,40]{1,0:T(4,128)}) custom-call(f32[4,40,3072]{2,1,0:T(8,128)S(1)} %get-tuple-element.17.late_ref, f32[8,160]{1,0:T(8,128)S(1)} %get-tuple-element.18.mine_ref, f32[8,160]{1,0:T(8,128)S(1)} %collective-permute-done.other_ref, f32[4,40,4096]{2,1,0:T(8,128)} %middle.1._), custom_call_target="tpu_custom_call", output_to_operand_aliasing={{0}: (3, {})} | custom-call | tf_op jit(solution)/shard_map/finish/pallas_call | solution.py:422
Async XLA Ops:
  4.9 41.4 %copy-start = (f32[256,128]{1,0:T(8,128)S(1)}, f32[256,128]{1,0:T(8,128)}, u32[]{:S(2)}) copy-start(f32[256,128]{1,0:T(8,128)} %constant.2.clone.table_ref) | copy-start | bytes 393220
  60.2 5.5 %collective-permute-start = (f32[8,160]{1,0:T(8,128)S(1)}, f32[8,160]{1,0:T(8,128)S(1)}, u32[]{:S(2)}, u32[]{:S(2)}) collective-permute-start(f32[8,160]{1,0:T(8,128)S(1)} %get-tuple-element.18.mine_ref), channel_id=1, source_target_pairs={{0,1},{1,0},{2,3},{3,2},{4,5},{5,4},{6,7},{7,6},{8,9},{9,8},{10,11... | collective-permute-start | bytes 15368 | tf_op jit(solution)/shard_map/ppermute | solution.py:410
